TPU v7x, 8 devices: a whole 2x2x1 slice. The times are simulated.
8 devices in a mesh: rep: 1 (over z), dp: 8 (over x, y, core).
Axes of the slice: x: 2, y: 2, z: 1, core: 2. Of those that a mesh axis runs over, the one named last changes fastest.
Arguments:
- x: bfloat16 [8, 2048, 1024], P(('rep', 'dp'))
- dy: bfloat16 [8, 2048, 1024], P(('rep', 'dp'))
- w_gate: bfloat16 [2, 1024, 3328], replicated
- w_up: bfloat16 [2, 1024, 3328], replicated
- w_down: bfloat16 [2, 3328, 1024], replicated
- m_w_gate: float32 [2, 1024, 3328], replicated
- m_w_up: float32 [2, 1024, 3328], replicated
- m_w_down: float32 [2, 3328, 1024], replicated
- v_w_gate: float32 [2, 1024, 3328], replicated
- v_w_up: float32 [2, 1024, 3328], replicated
- v_w_down: float32 [2, 3328, 1024], replicated
Outputs:
- output 1: bfloat16 [2, 1024, 3328], P('rep')
- output 2: bfloat16 [2, 1024, 3328], P('rep')
- output 3: bfloat16 [2, 3328, 1024], P('rep')
- output 4: float32 [2, 1024, 3328], P('rep')
- output 5: float32 [2, 1024, 3328], P('rep')
- output 6: float32 [2, 3328, 1024], P('rep')
- output 7: float32 [2, 1024, 3328], P('rep')
- output 8: float32 [2, 1024, 3328], P('rep')
- output 9: float32 [2, 3328, 1024], P('rep')
All inputs are finite; a program needn't handle non-finite values.
Results may differ from a plain program's by a relative error of at most 0.0229.
Values are sent between devices in bfloat16 or wider.
A program may use at most 2.75 GiB of HBM per device.

v0:
```python
import jax
import jax.numpy as jnp
from jax import lax
from jax.sharding import PartitionSpec as P

NAMES = ("w_gate", "w_up", "w_down")


def matmul(a, w):
    return jnp.dot(a, w, preferred_element_type=jnp.float32).astype(jnp.bfloat16)


def normed(h):
    wide = h.astype(jnp.float32)
    scale = lax.rsqrt(jnp.mean(wide**2, -1, keepdims=True) + 1e-6)
    return (wide * scale).astype(jnp.bfloat16)


def layer(h, w):
    a = normed(h)
    gate = jnp.dot(a, w["w_gate"], preferred_element_type=jnp.float32)
    up = jnp.dot(a, w["w_up"], preferred_element_type=jnp.float32)
    return h + matmul((jax.nn.silu(gate) * up).astype(jnp.bfloat16), w["w_down"])


def adamw(w, m, v, g):
    m = 0.9 * m + 0.1 * g
    v = 0.95 * v + 0.05 * g * g
    step = m * lax.rsqrt(v + 1e-8) + 0.1 * w
    return (w - 0.02 * step).astype(jnp.bfloat16), m, v


def solution(mesh):
    def step(x, dy, *arrays):
        weights, m, v = (arrays[i : i + 3] for i in (0, 3, 6))
        layers = weights[0].shape[0]
        h, kept = x[0], []
        for number in range(layers):
            kept.append(h)
            h = layer(h, {name: w[number] for name, w in zip(NAMES, weights, strict=True)})
        by_h, summed = dy[0], [None] * layers
        for number in reversed(range(layers)):
            _, back = jax.vjp(lambda w, h: layer(h, w), {name: w[number] for name, w in zip(NAMES, weights, strict=True)}, kept[number])
            by_w, by_h = back(by_h)
            summed[number] = [lax.psum(by_w[name], "dp") for name in NAMES]
        gradients = [jnp.stack([summed[number][i] for number in range(layers)]).astype(jnp.float32) for i in range(3)]
        new = [adamw(w.astype(jnp.float32), m, v, g) for w, m, v, g in zip(weights, m, v, gradients, strict=True)]
        return tuple(one[which] for which in range(3) for one in new)

    return jax.shard_map(
        step,
        mesh=mesh,
        in_specs=(P(("rep", "dp"), None, None),) * 2 + (P(None, None, None),) * 9,
        out_specs=(P("rep", None, None),) * 9,
        check_vma=False,
    )
```

profile of v0, /device:TPU:0, one launch (start us, length us, event | category | flops | bytes accessed | tf_op | source)
XLA Modules:
  0.0 1024.5 jit_solution(2629977033106253230)
XLA Ops:
  7.2 0.0 all-reduce.3.cloned.1.call-start
  7.2 6.6 copy.20
  13.8 3.1 fusion.30
  16.8 0.0 copy-start.5
  16.9 6.5 copy.21
  23.3 21.0 %convolution_convert_fusion.1 = bf16[2048,3328]{1,0:T(8,128)(2,1)} fusion(bf16[2,3328,1024]{2,1,0:T(8,128)(2,1)} %param.15, bf16[1,2048,1024]{2,1,0:T(8,128)(2,1)} %param.12), kind=kOutput, calls=%fused_computation.50 | convolution fusion | flops 13965459456 | bytes 24641536 | tf_op jit(solution)/shard_map/transpose(jvp())/dot_general | solution.py:10
  44.3 0.0 copy-start.2
  44.3 22.3 %fusion.56 = f32[2048,3328]{1,0:T(8,128)} fusion(bf16[2,1024,3328]{2,1,0:T(8,128)(2,1)} %param.13, bf16[1,2048,1024]{2,1,0:T(8,128)(2,1)} %param.11, f32[2048]{0:T(1024)S(1)} %add_rsqrt_fusion), kind=kOutput, calls=%fused_computation.90 | convolution fusion | flops 13964935168 | bytes 38281216 | tf_op jit(solution)/shard_map/dot_general | solution.py:21
  66.6 0.0 copy-done.5
  66.6 0.0 copy-done.2
  66.6 29.0 %multiply_convert_fusion.1 = (bf16[2048,3328]{1,0:T(8,128)(2,1)}, f32[2048,3328]{1,0:T(8,128)}) fusion(f32[2048,3328]{1,0:T(8,128)} %fusion.56, bf16[2,1024,3328]{2,1,0:T(8,128)(2,1)} %param.14, bf16[1,2048,1024]{2,1,0:T(8,128)(2,1)S(1)} %copy-done.2, f32[2048]{0:T(1024)S(1)} %add_rsqrt_fusion), kind=kOutput, calls=%fused_computation.44 | convolution fusion | flops 14005829632 | bytes 79175680 | tf_op jit(solution)/shard_map/dot_general | solution.py:22
  95.6 22.1 %fusion.34 = (f32[2048]{0:T(1024)S(1)}, bf16[2048,1024]{0,1:T(8,128)(2,1)}) fusion(bf16[2048,3328]{1,0:T(8,128)(2,1)} %get-tuple-element.24, bf16[2,3328,1024]{2,1,0:T(8,128)(2,1)} %param.15, bf16[1,2048,1024]{1,2,0:T(8,128)(2,1)} %copy.20), kind=kOutput, calls=%fused_computation.67 | convolution fusion | flops 13969127424 | bytes 28844032 | tf_op jit(solution)/shard_map/dot_general | solution.py:10
  117.7 0.0 copy-start.3
  117.7 23.8 %fusion.43 = f32[2048,3328]{1,0:T(8,128)} fusion(bf16[2,1024,3328]{2,1,0:T(8,128)(2,1)} %param.14, bf16[2048,1024]{0,1:T(8,128)(2,1)} %get-tuple-element.27, f32[2048]{0:T(1024)S(1)} %fusion.92), kind=kOutput, calls=%fused_computation.77 | convolution fusion | flops 13964935168 | bytes 38281216 | tf_op jit(solution)/shard_map/jvp()/dot_general | solution.py:22
  141.5 0.0 copy-done.3
  141.5 40.0 %fusion.14 = (bf16[2048,3328]{1,0:T(8,128)(2,1)}, f32[2048,3328]{1,0:T(8,128)}) fusion(f32[2048,3328]{1,0:T(8,128)} %fusion.43, bf16[2048,3328]{1,0:T(8,128)(2,1)} %convolution_convert_fusion.1, bf16[2,1024,3328]{2,1,0:T(8,128)(2,1)} %param.13, bf16[2048,1024]{0,1:T(8,128)(2,1)} %get-tuple-element.27, f32[2048]{0:T(1024)S(1)} %fusion.92), kind=kOutput, calls=%fused_computation.32 | convolution fusion | flops 14046724096 | bytes 92807168 | tf_op jit(solution)/shard_map/jvp()/dot_general | solution.py:21
  181.5 0.0 copy-start.1
  181.5 22.9 %fusion.27 = bf16[2048,1024]{0,1:T(8,128)(2,1)} fusion(bf16[2048,3328]{1,0:T(8,128)(2,1)} %convolution_convert_fusion.1, bf16[2,1024,3328]{2,1,0:T(8,128)(2,1)} %param.14, f32[2048,3328]{1,0:T(8,128)} %get-tuple-element.29), kind=kOutput, calls=%fused_computation.48 | convolution fusion | flops 13999538176 | bytes 51904512 | tf_op jit(solution)/shard_map/transpose(jvp())/dot_general | solution.py:22
  204.4 0.0 copy-done.1
  204.4 24.3 %fusion.64 = bf16[1,1024,3328]{2,1,0:T(8,128)(2,1)} fusion(bf16[2048,3328]{1,0:T(8,128)(2,1)} %convolution_convert_fusion.1, bf16[2048,1024]{0,1:T(8,128)(2,1)S(1)} %copy-done.1, f32[2048]{0:T(1024)S(1)} %fusion.92, f32[2048,3328]{1,0:T(8,128)} %get-tuple-element.29), kind=kOutput, calls=%fused_computation.98 | convolution fusion | flops 14009237504 | bytes 51912704 | tf_op jit(solution)/shard_map/transpose(jvp())/dot_general | solution.py:22
  228.7 26.9 %fusion.65 = bf16[1,3328,1024]{2,1,0:T(8,128)(2,1)} fusion(f32[2048,3328]{1,0:T(8,128)} %fusion.43, bf16[1,2048,1024]{2,1,0:T(8,128)(2,1)} %param.12, f32[2048,3328]{1,0:T(8,128)} %get-tuple-element.29), kind=kOutput, calls=%fused_computation.99 | convolution fusion | flops 14002946048 | bytes 65536000 | tf_op jit(solution)/shard_map/transpose(jvp())/dot_general | solution.py:10
  255.6 21.6 %fusion.61 = bf16[1,1024,3328]{2,1,0:T(8,128)(2,1)} fusion(bf16[2048,3328]{1,0:T(8,128)(2,1)} %get-tuple-element.28, bf16[2048,1024]{0,1:T(8,128)(2,1)} %get-tuple-element.27, f32[2048]{0:T(1024)S(1)} %fusion.92), kind=kOutput, calls=%fused_computation.95 | convolution fusion | flops 13964935168 | bytes 24649728 | tf_op jit(solution)/shard_map/transpose(jvp())/dot_general | solution.py:21
  277.2 0.0 copy-start.4
  277.3 22.8 %fusion.36 = (f32[2048]{0:T(1024)S(1)}, bf16[2048,1024]{0,1:T(8,128)(2,1)}) fusion(bf16[2048,1024]{0,1:T(8,128)(2,1)} %get-tuple-element.27, bf16[2048,1024]{0,1:T(8,128)(2,1)} %fusion.27, bf16[2048,3328]{1,0:T(8,128)(2,1)} %get-tuple-element.28, bf16[2,1024,3328]{2,1,0:T(8,128)(2,1)} %param.13), kind=kOutput, calls=%fused_computation.69 | convolution fusion | flops 13969127424 | bytes 33038336 | tf_op jit(solution)/shard_map/transpose(jvp())/dot_general | solution.py:21
  300.1 0.0 copy-done.4
  300.1 7.6 fusion.77
  307.7 21.2 %convolution_convert_fusion = bf16[2048,3328]{1,0:T(8,128)(2,1)} fusion(bf16[2048,1024]{0,1:T(8,128)(2,1)} %fusion.77, bf16[2,3328,1024]{2,1,0:T(8,128)(2,1)} %param.15), kind=kOutput, calls=%fused_computation.49 | convolution fusion | flops 13965459456 | bytes 24641536 | tf_op jit(solution)/shard_map/transpose(jvp())/dot_general | solution.py:10
  328.8 0.0 copy-start
  328.8 0.0 copy-start.6
  328.8 20.9 %fusion.62 = bf16[1,3328,1024]{2,1,0:T(8,128)(2,1)} fusion(bf16[2048,3328]{1,0:T(8,128)(2,1)} %get-tuple-element.24, bf16[2048,1024]{0,1:T(8,128)(2,1)} %fusion.77), kind=kOutput, calls=%fused_computation.96 | convolution fusion | flops 13962051584 | bytes 24641536 | tf_op jit(solution)/shard_map/transpose(jvp())/dot_general | solution.py:10
  349.8 0.0 copy-done
  349.8 0.0 copy-done.6
  349.8 24.4 %fusion.63 = bf16[1,1024,3328]{2,1,0:T(8,128)(2,1)} fusion(bf16[2048,3328]{1,0:T(8,128)(2,1)} %convolution_convert_fusion, f32[2048,3328]{1,0:T(8,128)} %fusion.56, bf16[1,2048,1024]{1,2,0:T(8,128)(2,1)S(1)} %copy-done, f32[2048]{0:T(1024)S(1)} %copy-done.6), kind=kOutput, calls=%fused_computation.97 | convolution fusion | flops 14009237504 | bytes 51912704 | tf_op jit(solution)/shard_map/transpose(jvp())/dot_general | solution.py:22
  374.2 31.0 %fusion.66 = bf16[1,1024,3328]{2,1,0:T(8,128)(2,1)} fusion(f32[2048,3328]{1,0:T(8,128)} %fusion.56, f32[2048,3328]{1,0:T(8,128)} %get-tuple-element.25, bf16[2048,3328]{1,0:T(8,128)(2,1)} %convolution_convert_fusion, bf16[1,2048,1024]{1,2,0:T(8,128)(2,1)} %copy.20, f32[2048]{0:T(1024)S(1)} %copy-done.6), kind=kOutput, calls=%fused_computation.100 | convolution fusion | flops 14043316224 | bytes 79175680 | tf_op jit(solution)/shard_map/transpose(jvp())/dot_general | solution.py:21
  405.2 0.0 all-reduce.3.cloned.1.call-update
  405.2 467.1 %all-reduce.3.cloned.1.call-done = (bf16[1,1024,3328]{2,1,0:T(8,128)(2,1)}, bf16[1,1024,3328]{2,1,0:T(8,128)(2,1)}, bf16[1,1024,3328]{2,1,0:T(8,128)(2,1)}, bf16...) async-done(((bf16[1,1024,3328]{2,1,0:T(8,128)(2,1)}, bf16[1,1024,3328]{2,1,0:T(8,128)(2,1)}, ...) | async-done | bytes 40894480 | tf_op jit(solution)/shard_map/psum | solution.py:45
  872.3 51.6 %fusion.11 = (bf16[2,3328,1024]{2,1,0:T(8,128)(2,1)}, f32[2,3328,1024]{2,1,0:T(8,128)}, f32[2,3328,1024]{2,1,0:T(8,128)}) fusion(bf16[2,3328,1024]{2,1,0:T(8,128)(2,1)} %param.15, bf16[1,3328,1024]{2,1,0:T(8,128)(2,1)} %get-tuple-element.13, bf16[1,3328,1024]{2,1,0:T(8,128)(2,1)} %get-tuple-element.14, f32[2,3328,1024]{2,1,0:T(8,128)} %param.21, ...), kind=kLoop, calls=%fused_computation.29 | loop fusion | flops 129499136 | bytes 149946368 | tf_op jit(solution)/shard_map/convert_element_type | solution.py:30
  923.9 93.3 %fusion.2 = (bf16[2,1024,3328]{2,1,0:T(8,128)(2,1)}, f32[2,1024,3328]{2,1,0:T(8,128)}, f32[2,1024,3328]{2,1,0:T(8,128)}, bf16[2,1024,3328]{2,1,0:T(8,128)(2,1)},...) fusion(bf16[2,1024,3328]{2,1,0:T(8,128)(2,1)} %param.13, bf16[1,1024,3328]{2,1,0:T(8,128)(2,1)} %get-tuple-element.9, ...), kind=kLoop, calls=%fused_computation.20 | loop fusion | flops 258998272 | bytes 299892736 | tf_op jit(solution)/shard_map/convert_element_type | solution.py:30
  (3 shorter events, 0.0 us)
Async XLA Ops:
  7.2 865.1 %all-reduce.3.cloned.1.call-start = ((), (), s32[]{:S(2)}) async-start(), calls=%async_computation | async-start | bytes 81788928 | tf_op jit(solution)/shard_map/psum | solution.py:45
  16.8 49.8 %copy-start.5 = (f32[2048]{0:T(1024)}, f32[2048]{0:T(1024)S(1)}, u32[]{:S(2)}) copy-start(f32[2048]{0:T(1024)S(1)} %add_rsqrt_fusion) | copy-start | bytes 24580
  44.3 22.3 %copy-start.2 = (bf16[1,2048,1024]{2,1,0:T(8,128)(2,1)S(1)}, bf16[1,2048,1024]{2,1,0:T(8,128)(2,1)}, u32[]{:S(2)}) copy-start(bf16[1,2048,1024]{2,1,0:T(8,128)(2,1)} %param.11) | copy-start | bytes 12582916
  117.7 23.8 %copy-start.3 = (f32[2048]{0:T(1024)}, f32[2048]{0:T(1024)S(1)}, u32[]{:S(2)}) copy-start(f32[2048]{0:T(1024)S(1)} %get-tuple-element.26) | copy-start | bytes 24580
  181.5 22.9 %copy-start.1 = (bf16[2048,1024]{0,1:T(8,128)(2,1)S(1)}, bf16[2048,1024]{0,1:T(8,128)(2,1)}, u32[]{:S(2)}) copy-start(bf16[2048,1024]{0,1:T(8,128)(2,1)} %get-tuple-element.27) | copy-start | bytes 12582916
  277.2 22.8 %copy-start.4 = (f32[2048]{0:T(1024)S(1)}, f32[2048]{0:T(1024)}, u32[]{:S(2)}) copy-start(f32[2048]{0:T(1024)} %copy-done.3) | copy-start | bytes 24580
  328.8 20.9 %copy-start = (bf16[1,2048,1024]{1,2,0:T(8,128)(2,1)S(1)}, bf16[1,2048,1024]{1,2,0:T(8,128)(2,1)}, u32[]{:S(2)}) copy-start(bf16[1,2048,1024]{1,2,0:T(8,128)(2,1)} %copy.20) | copy-start | bytes 12582916
  328.8 20.9 %copy-start.6 = (f32[2048]{0:T(1024)S(1)}, f32[2048]{0:T(1024)}, u32[]{:S(2)}) copy-start(f32[2048]{0:T(1024)} %copy-done.5) | copy-start | bytes 24580
Sparse Core Ops, SparseCore 0:
  405.3 466.9 all-reduce.2
where the time goes:
time: 1030 us; the launch traced here: 1020 us
  waiting for transfers between devices  467 us (45%)
  matrix products  374 us (36%)
  other arithmetic  156 us (15%)
  between operations  14.6 us (1%)
  local copies, waits for them, and re-layouts  13.1 us (1%)
    psum x1, waiting for transfers between devices, step(): summed[number] = [lax.psum(by_w[name], 'dp') for name in NAMES]  467 us
    convert_element_type x2, other arithmetic, adamw(): return ((w - 0.02 * step).astype(jnp.bfloat16), m, v)  145 us
    dot_general x5, matrix products, layer(): gate = jnp.dot(a, w['w_gate'], preferred_element_type=jnp.float32)  138 us
    dot_general x5, matrix products, layer(): up = jnp.dot(a, w['w_up'], preferred_element_type=jnp.float32)  124 us
    dot_general x5, matrix products, matmul(): jnp.dot(a, w, preferred_element_type=jnp.float32).astype(jnp.bfloat16)  112 us
  transfers between devices with their start and end apart: 1, of which 1 were waited for; matrix products, arithmetic and copies ran while one was open for 0% of the time, Pallas kernels for 0%

commit v1 on v0

v1 whole, which is shorter than its diff:
```python
import functools

import jax
import jax.numpy as jnp
from jax import lax
from jax.experimental import pallas as pl
from jax.experimental.pallas import tpu as pltpu
from jax.sharding import PartitionSpec as P

F32, BF16 = jnp.float32, jnp.bfloat16
T, D, FF = 2048, 1024, 3328
BLK = 256
NB = FF // BLK
CH = 512
EPS = 1e-6
MESH = pl.DeviceIdType.MESH
VMEM_LIMIT = 64 * 1024 * 1024 - 65536 - 1024 * 1024


def dot(a, b):
    return lax.dot_general(a, b, (((1,), (0,)), ((), ())), preferred_element_type=F32)


def dot_nt(a, b):
    return lax.dot_general(a, b, (((1,), (1,)), ((), ())), preferred_element_type=F32)


def whole(shape):
    return pl.BlockSpec(shape, lambda *_: (0,) * len(shape), pipeline_mode=pl.Buffered(1))


def norm_rows(h):
    wide = h.astype(F32)
    scale = lax.rsqrt(jnp.mean(wide * wide, -1, keepdims=True) + EPS)
    return (wide * scale).astype(BF16)


def forward_kernel(x_ref, wg_ref, wu_ref, wd_ref, gate_ref, up_ref, h_ref, a_ref, a0, acc):
    j = pl.program_id(0)

    @pl.when(j == 0)
    def _():
        def prepare(i, _):
            rows = pl.ds(pl.multiple_of(i * CH, CH), CH)
            a0[rows, :] = norm_rows(x_ref[rows, :])
            acc[rows, :] = jnp.zeros((CH, D), F32)
            return 0

        lax.fori_loop(0, T // CH, prepare, 0)

    def chunk(i, _):
        rows = pl.ds(pl.multiple_of(i * CH, CH), CH)
        a = a0[rows, :]
        g = dot(a, wg_ref[0])
        u = dot(a, wu_ref[0])
        gate_ref[rows, :] = g
        up_ref[rows, :] = u
        hid = (g * jax.nn.sigmoid(g) * u).astype(BF16)
        acc[rows, :] += dot(hid, wd_ref[0])
        return 0

    lax.fori_loop(0, T // CH, chunk, 0)

    @pl.when(j == NB - 1)
    def _():
        def finish(i, _):
            rows = pl.ds(pl.multiple_of(i * CH, CH), CH)
            h = (x_ref[rows, :].astype(F32) + acc[rows, :].astype(BF16).astype(F32)).astype(BF16)
            h_ref[rows, :] = h
            a_ref[rows, :] = norm_rows(h)
            return 0

        lax.fori_loop(0, T // CH, finish, 0)


def forward(x, wg, wu, wd):
    return pl.pallas_call(
        forward_kernel,
        grid=(NB,),
        in_specs=[
            whole((T, D)),
            pl.BlockSpec((1, D, BLK), lambda j: (0, 0, j)),
            pl.BlockSpec((1, D, BLK), lambda j: (0, 0, j)),
            pl.BlockSpec((1, BLK, D), lambda j: (0, j, 0)),
        ],
        out_specs=[
            pl.BlockSpec((T, BLK), lambda j: (0, j)),
            pl.BlockSpec((T, BLK), lambda j: (0, j)),
            whole((T, D)),
            whole((T, D)),
        ],
        out_shape=[
            jax.ShapeDtypeStruct((T, FF), F32),
            jax.ShapeDtypeStruct((T, FF), F32),
            jax.ShapeDtypeStruct((T, D), BF16),
            jax.ShapeDtypeStruct((T, D), BF16),
        ],
        scratch_shapes=[pltpu.VMEM((T, D), BF16), pltpu.VMEM((T, D), F32)],
        compiler_params=pltpu.CompilerParams(vmem_limit_bytes=VMEM_LIMIT),
        cost_estimate=pl.CostEstimate(flops=6 * T * D * FF, bytes_accessed=8 * T * FF, transcendentals=T * FF),
        name="fwd0",
    )(x, wg, wu, wd)


SLOTS = 3


def store_pieces(g_buf, q, value):
    value = value.astype(BF16)
    for c in range(2):
        for ab in range(2):
            for s1 in range(2):
                for s2 in range(2):
                    x, y = (s1, s2) if ab == 0 else (s2, s1)
                    d = x * 4 + y * 2 + c
                    if q < 2:
                        r = d * 128 + ab * 64
                        g_buf[c, ab, s1, s2, q] = value[r : r + 64]
                    else:
                        r = d * 32 + ab * 16
                        for k in range(4):
                            g_buf[c, ab, s1, s2, q, k * 16 : k * 16 + 16] = value[r : r + 16, k * 256 : k * 256 + 256]


class Exchange:
    def __init__(self, bufs, sems):
        self.g, self.h, self.q, self.r0, self.r1, self.r2 = bufs
        self.send, self.recv, self.ahead = sems
        me = lax.axis_index("dp")
        self.rep = lax.axis_index("rep")
        self.x, self.y, self.c = me // 4, (me // 2) % 2, me % 2
        self.nx = (1 - self.x) * 4 + self.y * 2 + self.c
        self.ny = self.x * 4 + (1 - self.y) * 2 + self.c
        self.nc = self.x * 4 + self.y * 2 + (1 - self.c)

    def copy(self, kind, block, src, dst, to):
        slot = lax.rem(block, SLOTS)
        return pltpu.make_async_remote_copy(
            src_ref=src,
            dst_ref=dst,
            send_sem=self.send.at[kind, slot],
            recv_sem=self.recv.at[kind, slot],
            device_id=(self.rep, to),
            device_id_type=MESH,
        )

    def pair(self, b):
        return [self.copy(0, b, self.g.at[1 - self.c], self.r0.at[lax.rem(b, SLOTS)], self.nc)]

    def first(self, b):
        s = lax.rem(b, SLOTS)
        return [
            self.copy(1, b, self.h.at[0, 1 - self.x], self.r1.at[s, 0], self.nx),
            self.copy(2, b, self.h.at[1, 1 - self.y], self.r1.at[s, 1], self.ny),
        ]

    def second(self, b):
        s = lax.rem(b, SLOTS)
        return [
            self.copy(3, b, self.q.at[0, 1 - self.y], self.r2.at[s, 0], self.ny),
            self.copy(4, b, self.q.at[1, 1 - self.x], self.r2.at[s, 1], self.nx),
        ]

    def greet(self):
        barrier = pltpu.get_barrier_semaphore()
        for n in (self.nx, self.ny, self.nc):
            pl.semaphore_signal(barrier, inc=1, device_id=(self.rep, n), device_id_type=MESH)
        pl.semaphore_wait(barrier, 3)

    def wait_peers(self, count=1):
        for k in range(3):
            pl.semaphore_wait(self.ahead.at[k], count)

    def tell_peers(self):
        for k, n in enumerate((self.nx, self.ny, self.nc)):
            pl.semaphore_signal(self.ahead.at[k], inc=1, device_id=(self.rep, n), device_id_type=MESH)

    def stages(self, t, e_ref):
        @pl.when(t >= 3)
        def _():
            b = t - 3
            s = lax.rem(b, SLOTS)
            for cp in self.second(b):
                cp.wait()
            for ab, s2 in ((0, self.y), (1, self.x)):
                e_ref[0, ab] = (self.q[ab, s2].astype(F32) + self.r2[s, ab].astype(F32)).astype(BF16)

        @pl.when((t >= 2) & (t < NB + 2))
        def _():
            b = t - 2
            s = lax.rem(b, SLOTS)
            for cp in self.first(b):
                cp.wait()
            for ab, s1 in ((0, self.x), (1, self.y)):
                for s2 in range(2):
                    self.q[ab, s2] = (self.h[ab, s1, s2].astype(F32) + self.r1[s, ab, s2].astype(F32)).astype(BF16)
            for cp in self.second(b):
                cp.start()

        @pl.when((t >= 1) & (t < NB + 1))
        def _():
            b = t - 1
            s = lax.rem(b, SLOTS)
            for cp in self.pair(b):
                cp.wait()

            def add(k, _):
                ab, s1, s2 = k // 4, (k // 2) % 2, k % 2
                self.h[ab, s1, s2] = (self.g[self.c, ab, s1, s2].astype(F32) + self.r0[s, ab, s1, s2].astype(F32)).astype(BF16)
                return 0

            lax.fori_loop(0, 8, add, 0)
            for cp in self.first(b):
                cp.start()


EXCHANGE_SCRATCH = [
    pltpu.VMEM((2, 2, 2, 2, 3, 64, BLK), BF16),
    pltpu.VMEM((2, 2, 2, 3, 64, BLK), BF16),
    pltpu.VMEM((2, 2, 3, 64, BLK), BF16),
    pltpu.VMEM((SLOTS, 2, 2, 2, 3, 64, BLK), BF16),
    pltpu.VMEM((SLOTS, 2, 2, 3, 64, BLK), BF16),
    pltpu.VMEM((SLOTS, 2, 3, 64, BLK), BF16),
    pltpu.SemaphoreType.DMA((5, SLOTS)),
    pltpu.SemaphoreType.DMA((5, SLOTS)),
    pltpu.SemaphoreType.REGULAR((3,)),
]
STEPS = NB + 3


def gate_grads(g, u, dh):
    s = jax.nn.sigmoid(g)
    sg = g * s
    hid = (sg * u).astype(BF16)
    dh = dh.astype(BF16).astype(F32)
    dgate = (dh * u * (s * (1.0 + g * (1.0 - s)))).astype(BF16)
    dup = (dh * sg).astype(BF16)
    return hid, dgate, dup


def weight_grads(ex, at_ref, dt_ref, hid_s, dg_s, du_s):
    store_pieces(ex.g, 0, dot(at_ref[...], dg_s[...]))
    store_pieces(ex.g, 1, dot(at_ref[...], du_s[...]))
    store_pieces(ex.g, 2, dot(dt_ref[...], hid_s[...]).T)


def around(ex, e_ref, compute):
    t = pl.program_id(0)

    @pl.when(t == 0)
    def _():
        ex.greet()

    @pl.when(t >= 2)
    def _():
        ex.wait_peers()

    ex.stages(t, e_ref)

    @pl.when(t < NB)
    def _():
        compute(t)
        for cp in ex.pair(t):
            cp.start()

    ex.tell_peers()

    @pl.when(t == STEPS - 1)
    def _():
        ex.wait_peers(2)


def last_layer_kernel(a_ref, at_ref, dy_ref, dyt_ref, h_ref, wg_ref, wu_ref, wd_ref, e_ref, dh_ref, acc, hid_s, dg_s, du_s, *scratch):
    ex = Exchange(scratch[:6], scratch[6:])

    def compute(t):
        @pl.when(t == 0)
        def _():
            acc[...] = jnp.zeros((T, D), F32)

        def chunk(i, _):
            rows = pl.ds(pl.multiple_of(i * CH, CH), CH)
            a = a_ref[rows, :]
            g = dot(a, wg_ref[0])
            u = dot(a, wu_ref[0])
            dh = dot_nt(dy_ref[rows, :], wd_ref[0])
            hid, dgate, dup = gate_grads(g, u, dh)
            hid_s[rows, :] = hid
            dg_s[rows, :] = dgate
            du_s[rows, :] = dup
            acc[rows, :] += dot_nt(dgate, wg_ref[0]) + dot_nt(dup, wu_ref[0])
            return 0

        lax.fori_loop(0, T // CH, chunk, 0)
        weight_grads(ex, at_ref, dyt_ref, hid_s, dg_s, du_s)

    around(ex, e_ref, compute)

    @pl.when(pl.program_id(0) == NB)
    def _():
        def chunk(i, _):
            rows = pl.ds(pl.multiple_of(i * CH, CH), CH)
            wide = h_ref[rows, :].astype(F32)
            da = acc[rows, :].astype(BF16).astype(F32)
            scale = lax.rsqrt(jnp.mean(wide * wide, -1, keepdims=True) + EPS)
            inner = jnp.mean(da * wide, -1, keepdims=True)
            back = (da * scale - wide * (scale * scale * scale * inner)).astype(BF16)
            dh_ref[rows, :] = (dy_ref[rows, :].astype(F32) + back.astype(F32)).astype(BF16)
            return 0

        lax.fori_loop(0, T // CH, chunk, 0)


def first_layer_kernel(at_ref, dh_ref, dht_ref, gate_ref, up_ref, wd_ref, e_ref, hid_s, dg_s, du_s, *scratch):
    ex = Exchange(scratch[:6], scratch[6:])

    def compute(t):
        def chunk(i, _):
            rows = pl.ds(pl.multiple_of(i * CH, CH), CH)
            dh = dot_nt(dh_ref[rows, :], wd_ref[0])
            hid, dgate, dup = gate_grads(gate_ref[rows, :], up_ref[rows, :], dh)
            hid_s[rows, :] = hid
            dg_s[rows, :] = dgate
            du_s[rows, :] = dup
            return 0

        lax.fori_loop(0, T // CH, chunk, 0)
        weight_grads(ex, at_ref, dht_ref, hid_s, dg_s, du_s)

    around(ex, e_ref, compute)


def at_step(t):
    return jnp.minimum(t, NB - 1)


PIECES = (2, 3, 64, BLK)
E_SPEC = pl.BlockSpec((1,) + PIECES, lambda t: (jnp.maximum(t - 3, 0), 0, 0, 0, 0))
E_SHAPE = jax.ShapeDtypeStruct((NB,) + PIECES, BF16)
HALVES = [pltpu.VMEM((T, BLK), BF16)] * 3


def last_layer(a, at, dy, dyt, h, wg, wu, wd):
    return pl.pallas_call(
        last_layer_kernel,
        grid=(STEPS,),
        in_specs=[
            whole((T, D)),
            whole((D, T)),
            whole((T, D)),
            whole((D, T)),
            whole((T, D)),
            pl.BlockSpec((1, D, BLK), lambda t: (1, 0, at_step(t))),
            pl.BlockSpec((1, D, BLK), lambda t: (1, 0, at_step(t))),
            pl.BlockSpec((1, BLK, D), lambda t: (1, at_step(t), 0)),
        ],
        out_specs=[E_SPEC, whole((T, D))],
        out_shape=[E_SHAPE, jax.ShapeDtypeStruct((T, D), BF16)],
        scratch_shapes=[pltpu.VMEM((T, D), F32), *HALVES, *EXCHANGE_SCRATCH],
        compiler_params=pltpu.CompilerParams(vmem_limit_bytes=VMEM_LIMIT, collective_id=0, has_side_effects=True),
        cost_estimate=pl.CostEstimate(flops=16 * T * D * FF, bytes_accessed=6 * D * FF, transcendentals=T * FF),
        name="last_layer",
    )(a, at, dy, dyt, h, wg, wu, wd)


def first_layer(at, dh, dht, gate, up, wd):
    return pl.pallas_call(
        first_layer_kernel,
        grid=(STEPS,),
        in_specs=[
            whole((D, T)),
            whole((T, D)),
            whole((D, T)),
            pl.BlockSpec((T, BLK), lambda t: (0, at_step(t))),
            pl.BlockSpec((T, BLK), lambda t: (0, at_step(t))),
            pl.BlockSpec((1, BLK, D), lambda t: (0, at_step(t), 0)),
        ],
        out_specs=[E_SPEC],
        out_shape=[E_SHAPE],
        scratch_shapes=[*HALVES, *EXCHANGE_SCRATCH],
        compiler_params=pltpu.CompilerParams(vmem_limit_bytes=VMEM_LIMIT, collective_id=1, has_side_effects=True),
        cost_estimate=pl.CostEstimate(flops=8 * T * D * FF, bytes_accessed=8 * T * FF, transcendentals=T * FF),
        name="first_layer",
    )(at, dh, dht, gate, up, wd)[0]


def adamw(w, m, v, g):
    m = 0.9 * m + 0.1 * g
    v = 0.95 * v + 0.05 * g * g
    step = m * lax.rsqrt(v + 1e-8) + 0.1 * w
    return (w - 0.02 * step).astype(BF16), m, v


def adamw_kernel(g_ref, *refs):
    ins, outs = refs[:9], refs[-9:]
    for q in range(3):
        w_ref, m_ref, v_ref = ins[q], ins[3 + q], ins[6 + q]
        wo_ref, mo_ref, vo_ref = outs[q], outs[3 + q], outs[6 + q]
        if q < 2:
            for d in range(8):
                for ab in range(2):
                    r = pl.ds(d * 128 + ab * 64, 64)
                    g = g_ref[d, 0, ab, q].astype(F32)
                    wo_ref[0, r, :], mo_ref[0, r, :], vo_ref[0, r, :] = adamw(w_ref[0, r, :].astype(F32), m_ref[0, r, :], v_ref[0, r, :], g)
        else:
            for d in range(8):
                for ab in range(2):
                    r = pl.ds(d * 32 + ab * 16, 16)
                    for k in range(4):
                        c = pl.ds(k * 256, 256)
                        g = g_ref[d, 0, ab, q, k * 16 : k * 16 + 16].astype(F32)
                        wo_ref[0, r, c], mo_ref[0, r, c], vo_ref[0, r, c] = adamw(
                            w_ref[0, r, c].astype(F32), m_ref[0, r, c], v_ref[0, r, c], g
                        )


def update(layer, g, arrays, before):
    wide = pl.BlockSpec((1, D, BLK), lambda j: (layer, 0, j))
    tall = pl.BlockSpec((1, BLK, D), lambda j: (layer, j, 0))
    specs = [wide, wide, tall] * 3
    shapes = [jax.ShapeDtypeStruct(a.shape, a.dtype) for a in arrays]
    held = [] if before is None else list(before)
    return pl.pallas_call(
        adamw_kernel,
        grid=(NB,),
        in_specs=[pl.BlockSpec((8, 1) + PIECES, lambda j: (0, j, 0, 0, 0, 0)), *specs, *[pl.BlockSpec(memory_space=pl.ANY)] * len(held)],
        out_specs=specs,
        out_shape=shapes,
        input_output_aliases={10 + i: i for i in range(len(held))},
        compiler_params=pltpu.CompilerParams(vmem_limit_bytes=VMEM_LIMIT),
        cost_estimate=pl.CostEstimate(flops=30 * 3 * D * FF, bytes_accessed=22 * 3 * D * FF, transcendentals=3 * D * FF),
        name=f"adamw{layer}",
    )(g, *arrays, *held)


def solution(mesh):
    def step(x, dy, wg, wu, wd, *moments):
        x, dy = x[0], dy[0]
        gate, up, h1, a1 = forward(x, wg, wu, wd)
        e1, dh1 = last_layer(a1, a1.T, dy, dy.T, h1, wg, wu, wd)
        g1 = lax.all_gather(e1, "dp", axis=0, tiled=False)
        e0 = first_layer(norm_rows(x).T, dh1, dh1.T, gate, up, wd)
        g0 = lax.all_gather(e0, "dp", axis=0, tiled=False)
        arrays = (wg, wu, wd, *moments)
        g1, e0 = lax.optimization_barrier((g1, e0))
        new = update(1, g1, arrays, None)
        return tuple(update(0, g0, arrays, new))

    return jax.shard_map(
        step,
        mesh=mesh,
        in_specs=(P(("rep", "dp"), None, None),) * 2 + (P(None, None, None),) * 9,
        out_specs=(P("rep", None, None),) * 9,
        check_vma=False,
    )
```

time: 1030 us -> 689 us (0.67)
  Pallas kernels: 0 us -> 613 us
  waiting for transfers between devices: 467 us -> 26.1 us
  matrix products: 374 us -> 0 us
  other arithmetic: 156 us -> 8.64 us
  local copies, waits for them, and re-layouts: 13.1 us -> 25.7 us
    pallas_call x0 -> x5, Pallas kernels: none -> 613 us  [the longest x1 236 us: last_layer(): pl.pallas_call(last_layer_kernel, grid=(STEPS,), in_specs=[whole((T, D)),...]
    psum x1 -> x0, waiting for transfers between devices: 467 us -> none  [step(): summed[number] = [lax.psum(by_w[name], 'dp') for name in NAMES]]
    dot_general x15 -> x0, matrix products: 374 us -> none  [the longest x5 138 us: layer(): gate = jnp.dot(a, w['w_gate'], preferred_element_type=jnp.float32)]
    convert_element_type x2 -> x0, other arithmetic: 145 us -> none  [adamw(): return ((w - 0.02 * step).astype(jnp.bfloat16), m, v)]
    all_gather x0 -> x2, waiting for transfers between devices: none -> 26 us  [the longest x1 26 us: step(): g0 = lax.all_gather(e0, 'dp', axis=0, tiled=False)]
    pallas_call x0 -> x2, local copies, waits for them, and re-layouts: none -> 12.9 us  [the longest x1 6.43 us: forward(): pl.pallas_call(forward_kernel, grid=(NB,), in_specs=[whole((T, D)), pl.Bl...]
  transfers between devices with their start and end apart: 1 -> 2, of which waited for: 1 -> 1; matrix products, arithmetic and copies ran while one was open for 0% -> 3% of each run, Pallas kernels for 0% -> 35%
where the time goes in v1:
time: 689 us; the launch traced here: 688 us
  Pallas kernels  613 us (89%)
  waiting for transfers between devices  26.1 us (4%)
  local copies, waits for them, and re-layouts  25.7 us (4%)
  between operations  14.1 us (2%)
  other arithmetic  8.64 us (1%)
    pallas_call x1, Pallas kernels, last_layer(): pl.pallas_call(last_layer_kernel, grid=(STEPS,), in_specs=[whole((T, D)),...  236 us
    pallas_call x1, Pallas kernels, first_layer(): pl.pallas_call(first_layer_kernel, grid=(STEPS,), in_specs=[whole((D, T))...  166 us
    pallas_call x2, Pallas kernels, update(): pl.pallas_call(adamw_kernel, grid=(NB,), in_specs=[pl.BlockSpec((8, 1) +...  148 us
    pallas_call x1, Pallas kernels, forward(): pl.pallas_call(forward_kernel, grid=(NB,), in_specs=[whole((T, D)), pl.Bl...  63.3 us
    all_gather x1, waiting for transfers between devices, step(): g0 = lax.all_gather(e0, 'dp', axis=0, tiled=False)  26 us
  transfers between devices with their start and end apart: 2, of which 1 were waited for; matrix products, arithmetic and copies ran while one was open for 3% of the time, Pallas kernels for 35%

profile of v1, /device:TPU:0, one launch (start us, length us, event | category | flops | bytes accessed | tf_op | source)
XLA Modules:
  0.0 687.9 jit_solution(7337584504892325104)
XLA Ops:
  7.2 0.0 all-gather.7.cloned.1.call-start
  7.2 6.4 copy.38
  13.7 63.3 %fwd0.1 = (f32[2048,3328]{1,0:T(8,128)}, f32[2048,3328]{1,0:T(8,128)}, bf16[2048,1024]{1,0:T(8,128)(2,1)}, bf16[2048,1024]{1,0:T(8,128)(2,1)}) custom-call(bf16[2048,1024]{1,0:T(8,128)(2,1)} %bitcast.17, bf16[2,1024,3328]{2,1,0:T(8,128)(2,1)} %refs_0_.3, bf16[2,1024,3328]{2,1,0:T(8,128)(2,1)} %refs_1_.3, bf16[2,3328,1024]{2,1,0:T(8,128)(2,1)} %refs_2_.3), custom_call_target="tpu_custom_call" | custom-call | flops 41875931136 | bytes 54525952 | tf_op jit(solution)/shard_map/fwd0/pallas_call | solution.py:77
  77.0 6.4 copy.37
  83.4 236.3 %last_layer.1 = (bf16[13,2,3,64,256]{4,3,2,1,0:T(8,128)(2,1)}, bf16[2048,1024]{1,0:T(8,128)(2,1)}) custom-call(bf16[2048,1024]{1,0:T(8,128)(2,1)} %get-tuple-element.25.a_ref, bf16[1024,2048]{1,0:T(8,128)(2,1)} %bitcast.20, bf16[2048,1024]{1,0:T(8,128)(2,1)} %bitcast.16, bf16[1024,2048]{1,0:T(8,128)(2,1)} %bitcast.19, ...), custom_call_target="tpu_custom_call" | custom-call | flops 111669149696 | bytes 20447232 | tf_op jit(solution)/shard_map/last_layer/pallas_call | solution.py:344
  319.7 0.0 all-gather.7.cloned.1.call-update
  319.8 0.2 all-gather.5.cloned.1.call-start
  320.0 6.4 copy.35
  326.4 6.4 copy.40
  332.8 3.1 fusion
  335.9 5.6 fusion.2.at_ref
  341.5 165.8 %first_layer.1 = bf16[13,2,3,64,256]{4,3,2,1,0:T(8,128)(2,1)} custom-call(bf16[1024,2048]{1,0:T(8,128)(2,1)} %fusion.2.at_ref, bf16[2048,1024]{1,0:T(8,128)(2,1)} %get-tuple-element.27.dh_ref, bf16[1024,2048]{1,0:T(8,128)(2,1)} %bitcast.18, f32[2048,3328]{1,0:T(8,128)} %get-tuple-element.28.gate_ref, f32[2048,3328]{1,0:T(8,128)} %get-tuple-element.29.up_ref, ...), custom_call_target="tpu_custom_call" | custom-call | flops 55834574848 | bytes 54525952 | tf_op jit(solution)/shard_map/first_layer/pallas_call | solution.py:367
  507.3 0.0 all-gather.5.cloned.1.call-update
  507.4 0.0 all-gather.7.cloned.1.call-done
  507.4 73.8 %adamw1.1 = (bf16[2,1024,3328]{2,1,0:T(8,128)(2,1)}, bf16[2,1024,3328]{2,1,0:T(8,128)(2,1)}, bf16[2,3328,1024]{2,1,0:T(8,128)(2,1)}, f32[2,1024,3328]{2,1,0:T(8,...) custom-call(bf16[8,13,2,3,64,256]{5,4,3,2,1,0:T(8,128)(2,1)} %bitcas, ...), custom_call_target="tpu_custom_call" | custom-call | flops 306708480 | bytes 224919552 | tf_op jit(solution)/shard_map/adamw1/pallas_call | solution.py:423
  581.1 26.0 %all-gather.5.cloned.1.call-done = bf16[104,2,3,64,256]{4,3,2,1,0:T(8,128)(2,1)} async-done(((bf16[13,2,3,64,256]{4,3,2,1,0:T(8,128)(2,1)}), bf16[104,2,3,64,256]{4,3,2,1,0:T(8,128)(2,1)}) %all-gather.5.cloned.1.call-update) | async-done | bytes 20447248 | tf_op jit(solution)/shard_map/all_gather | solution.py:443
  607.1 73.9 %adamw0.1 = (bf16[2,1024,3328]{2,1,0:T(8,128)(2,1)}, bf16[2,1024,3328]{2,1,0:T(8,128)(2,1)}, bf16[2,3328,1024]{2,1,0:T(8,128)(2,1)}, f32[2,1024,3328]{2,1,0:T(8,...) custom-call(bf16[8,13,2,3,64,256]{5,4,3,2,1,0:T(8,128)(2,1)} %bitcas, ...), custom_call_target="tpu_custom_call", output_to_operand_aliasing={{0}: (10, {}), {1}: (11, {}), {2}: (12, {}), {3}: (13, {}),... | custom-call | flops 306708480 | bytes 224919552 | tf_op jit(solution)/shard_map/adamw0/pallas_call | solution.py:423
  (1 shorter events, 0.0 us)
Async XLA Ops:
  7.2 500.2 %all-gather.7.cloned.1.call-start = ((), (), s32[]{:S(2)}) async-start(), calls=%async_computation.1 | async-start | bytes 23003136 | tf_op jit(solution)/shard_map/all_gather | solution.py:441
  319.8 287.4 %all-gather.5.cloned.1.call-start = ((), (), s32[]{:S(2)}) async-start(), calls=%async_computation | async-start | bytes 23003136 | tf_op jit(solution)/shard_map/all_gather | solution.py:443
Sparse Core Ops, SparseCore 0:
  319.9 142.7 all-gather.6
  507.5 99.6 all-gather.4

commit v2 on v1

v2 whole, which is shorter than its diff:
```python
import functools
import itertools

import jax
import jax.numpy as jnp
from jax import lax
from jax.experimental import pallas as pl
from jax.experimental.pallas import tpu as pltpu
from jax.sharding import PartitionSpec as P

F32, BF16 = jnp.float32, jnp.bfloat16
T, D, FF = 2048, 1024, 3328
BLK = 256
NB = FF // BLK
CH = 512
TURN = 256
EPS = 1e-6
MESH = pl.DeviceIdType.MESH
VMEM_LIMIT = 64 * 1024 * 1024 - 65536 - 1024 * 1024


def dot(a, b):
    return lax.dot_general(a, b, (((1,), (0,)), ((), ())), preferred_element_type=F32)


def dot_nt(a, b):
    return lax.dot_general(a, b, (((1,), (1,)), ((), ())), preferred_element_type=F32)


def whole(shape):
    return pl.BlockSpec(shape, lambda *_: (0,) * len(shape), pipeline_mode=pl.Buffered(1))


def norm_rows(h):
    wide = h.astype(F32)
    scale = lax.rsqrt(jnp.mean(wide * wide, -1, keepdims=True) + EPS)
    return (wide * scale).astype(BF16)


def turn_step(j):
    return jnp.minimum(j, T // TURN - 1)


def pipelined(front, back):
    chunks = [pl.ds(i * CH, CH) for i in range(T // CH)]
    front(chunks[0])
    for i, rows in enumerate(chunks):
        if i + 1 < len(chunks):
            front(chunks[i + 1])
        back(rows)


def forward_kernel(x_ref, dy_ref, wg_ref, wu_ref, wd_ref, gate_ref, up_ref, h_ref, a_ref, at_ref, dyt_ref, a0, acc):
    j = pl.program_id(0)

    @pl.when(j == 0)
    def _():
        def prepare(i, _):
            rows = pl.ds(pl.multiple_of(i * CH, CH), CH)
            a0[rows, :] = norm_rows(x_ref[rows, :])
            acc[rows, :] = jnp.zeros((CH, D), F32)
            return 0

        lax.fori_loop(0, T // CH, prepare, 0)

    def front(rows):
        a = a0[rows, :]
        gate_ref[rows, :] = dot(a, wg_ref[0])
        up_ref[rows, :] = dot(a, wu_ref[0])

    def back(rows):
        g = gate_ref[rows, :]
        hid = (g * jax.nn.sigmoid(g) * up_ref[rows, :]).astype(BF16)
        acc[rows, :] += dot(hid, wd_ref[0])

    at_ref[...] = a0[pl.ds(pl.multiple_of(turn_step(j) * TURN, TURN), TURN), :].T
    dyt_ref[...] = dy_ref[...].T
    pipelined(front, back)

    @pl.when(j == NB - 1)
    def _():
        def finish(i, _):
            rows = pl.ds(pl.multiple_of(i * CH, CH), CH)
            h = (x_ref[rows, :].astype(F32) + acc[rows, :].astype(BF16).astype(F32)).astype(BF16)
            h_ref[rows, :] = h
            a_ref[rows, :] = norm_rows(h)
            return 0

        lax.fori_loop(0, T // CH, finish, 0)


def forward(x, dy, wg, wu, wd):
    return pl.pallas_call(
        forward_kernel,
        grid=(NB,),
        in_specs=[
            whole((T, D)),
            pl.BlockSpec((TURN, D), lambda j: (turn_step(j), 0)),
            pl.BlockSpec((1, D, BLK), lambda j: (0, 0, j)),
            pl.BlockSpec((1, D, BLK), lambda j: (0, 0, j)),
            pl.BlockSpec((1, BLK, D), lambda j: (0, j, 0)),
        ],
        out_specs=[
            pl.BlockSpec((T, BLK), lambda j: (0, j)),
            pl.BlockSpec((T, BLK), lambda j: (0, j)),
            whole((T, D)),
            whole((T, D)),
            pl.BlockSpec((D, TURN), lambda j: (0, turn_step(j))),
            pl.BlockSpec((D, TURN), lambda j: (0, turn_step(j))),
        ],
        out_shape=[
            jax.ShapeDtypeStruct((T, FF), F32),
            jax.ShapeDtypeStruct((T, FF), F32),
            jax.ShapeDtypeStruct((T, D), BF16),
            jax.ShapeDtypeStruct((T, D), BF16),
            jax.ShapeDtypeStruct((D, T), BF16),
            jax.ShapeDtypeStruct((D, T), BF16),
        ],
        scratch_shapes=[pltpu.VMEM((T, D), BF16), pltpu.VMEM((T, D), F32)],
        compiler_params=pltpu.CompilerParams(vmem_limit_bytes=VMEM_LIMIT),
        cost_estimate=pl.CostEstimate(flops=6 * T * D * FF, bytes_accessed=8 * T * FF, transcendentals=T * FF),
        name="fwd0",
    )(x, dy, wg, wu, wd)


SLOTS = 3


def store_pieces(g_buf, slot, q, value):
    value = value.astype(BF16)
    for c in range(2):
        for ab in range(2):
            for s1 in range(2):
                for s2 in range(2):
                    x, y = (s1, s2) if ab == 0 else (s2, s1)
                    d = x * 4 + y * 2 + c
                    if q < 2:
                        r = d * 128 + ab * 64
                        g_buf[slot, c, ab, s1, s2, q] = value[r : r + 64]
                    else:
                        r = d * 32 + ab * 16
                        for k in range(4):
                            g_buf[slot, c, ab, s1, s2, q, k * 16 : k * 16 + 16] = value[r : r + 16, k * 256 : k * 256 + 256]


class Exchange:
    def __init__(self, scratch, f=None):
        self.g, self.h, self.q, self.e, self.r0, self.r1, self.r2 = scratch[:7]
        self.send, self.recv, self.keep, self.ahead = scratch[7:]
        self.f = f
        me = lax.axis_index("dp")
        self.rep = lax.axis_index("rep")
        self.x, self.y, self.c = me // 4, (me // 2) % 2, me % 2
        self.nx = (1 - self.x) * 4 + self.y * 2 + self.c
        self.ny = self.x * 4 + (1 - self.y) * 2 + self.c
        self.nc = self.x * 4 + self.y * 2 + (1 - self.c)

    def copy(self, kind, block, src, dst, to):
        slot = lax.rem(block, SLOTS)
        return pltpu.make_async_remote_copy(
            src_ref=src,
            dst_ref=dst,
            send_sem=self.send.at[kind, slot],
            recv_sem=self.recv.at[kind, slot],
            device_id=(self.rep, to),
            device_id_type=MESH,
        )

    def pair(self, b):
        return [self.copy(0, b, self.g.at[lax.rem(b, 2), 1 - self.c], self.r0.at[lax.rem(b, SLOTS)], self.nc)]

    def first(self, b):
        s = lax.rem(b, SLOTS)
        return [
            self.copy(1, b, self.h.at[0, 1 - self.x], self.r1.at[s, 0], self.nx),
            self.copy(2, b, self.h.at[1, 1 - self.y], self.r1.at[s, 1], self.ny),
        ]

    def second(self, b):
        s = lax.rem(b, SLOTS)
        return [
            self.copy(3, b, self.q.at[0, 1 - self.y], self.r2.at[s, 0], self.ny),
            self.copy(4, b, self.q.at[1, 1 - self.x], self.r2.at[s, 1], self.nx),
        ]

    def greet(self):
        barrier = pltpu.get_barrier_semaphore()
        for n in (self.nx, self.ny, self.nc):
            pl.semaphore_signal(barrier, inc=1, device_id=(self.rep, n), device_id_type=MESH)
        pl.semaphore_wait(barrier, 3)

    def wait_peers(self, count=1):
        for k in range(3):
            pl.semaphore_wait(self.ahead.at[k], count)

    def tell_peers(self):
        for k, n in enumerate((self.nx, self.ny, self.nc)):
            pl.semaphore_signal(self.ahead.at[k], inc=1, device_id=(self.rep, n), device_id_type=MESH)

    def mine(self, ab):
        return (self.x, self.y) if ab == 0 else (self.y, self.x)

    def own(self, b):
        return [pltpu.make_async_copy(self.e.at[ab], self.f.at[(b, self.c, ab, *self.mine(ab))], self.keep.at[ab]) for ab in range(2)]

    def back_first(self, b):
        return [self.copy(5 + ab, b, self.e.at[ab], self.f.at[(b, self.c, ab, *self.mine(ab))], (self.ny, self.nx)[ab]) for ab in range(2)]

    def back_second(self, b):
        out = []
        for ab in range(2):
            part = self.f.at[b, self.c, ab, self.mine(ab)[0]]
            out.append(self.copy(7 + ab, b, part, part, (self.nx, self.ny)[ab]))
        return out

    def back_pair(self, b):
        return [self.copy(9, b, self.f.at[b, self.c], self.f.at[b, self.c], self.nc)]

    def sums(self, b, out):
        s = lax.rem(b, SLOTS)
        for ab in range(2):
            s2 = self.mine(ab)[1]
            out[ab] = (self.q[ab, s2].astype(F32) + self.r2[s, ab].astype(F32)).astype(BF16)

    def stages(self, t, gathered, e_refs):
        def at(lag, end, begin=0):
            return (t >= begin + lag) & (t < end + lag)

        if gathered:

            @pl.when(at(6, gathered))
            def _():
                for cp in self.back_pair(t - 6):
                    cp.wait()

            @pl.when(at(5, gathered))
            def _():
                for cp in self.back_second(t - 5):
                    cp.wait()
                for cp in self.back_pair(t - 5):
                    cp.start()

            @pl.when(at(4, gathered))
            def _():
                for cp in self.own(t - 4) + self.back_first(t - 4):
                    cp.wait()
                for cp in self.back_second(t - 4):
                    cp.start()

        @pl.when(at(3, NB))
        def _():
            for cp in self.second(t - 3):
                cp.wait()

        if gathered:

            @pl.when(at(3, gathered))
            def _():
                b = t - 3
                self.sums(b, self.e)
                for cp in self.own(b) + self.back_first(b):
                    cp.start()

        for begin, end, e_ref in e_refs:

            @pl.when(at(3, end, begin))
            def _(e_ref=e_ref):
                self.sums(t - 3, e_ref.at[0])

        @pl.when(at(2, NB))
        def _():
            b = t - 2
            s = lax.rem(b, SLOTS)
            for cp in self.first(b):
                cp.wait()
            for ab in range(2):
                s1 = self.mine(ab)[0]
                for s2 in range(2):
                    self.q[ab, s2] = (self.h[ab, s1, s2].astype(F32) + self.r1[s, ab, s2].astype(F32)).astype(BF16)
            for cp in self.second(b):
                cp.start()

        @pl.when(at(1, NB))
        def _():
            b = t - 1
            s = lax.rem(b, SLOTS)
            g = lax.rem(b, 2)
            for cp in self.pair(b):
                cp.wait()

            def add(k, _):
                ab, s1, s2 = k // 4, (k // 2) % 2, k % 2
                self.h[ab, s1, s2] = (self.g[g, self.c, ab, s1, s2].astype(F32) + self.r0[s, ab, s1, s2].astype(F32)).astype(BF16)
                return 0

            lax.fori_loop(0, 8, add, 0)
            for cp in self.first(b):
                cp.start()


EXCHANGE_SCRATCH = [
    pltpu.VMEM((2, 2, 2, 2, 2, 3, 64, BLK), BF16),
    pltpu.VMEM((2, 2, 2, 3, 64, BLK), BF16),
    pltpu.VMEM((2, 2, 3, 64, BLK), BF16),
    pltpu.VMEM((2, 3, 64, BLK), BF16),
    pltpu.VMEM((SLOTS, 2, 2, 2, 3, 64, BLK), BF16),
    pltpu.VMEM((SLOTS, 2, 2, 3, 64, BLK), BF16),
    pltpu.VMEM((SLOTS, 2, 3, 64, BLK), BF16),
    pltpu.SemaphoreType.DMA((10, SLOTS)),
    pltpu.SemaphoreType.DMA((10, SLOTS)),
    pltpu.SemaphoreType.DMA((2,)),
    pltpu.SemaphoreType.REGULAR((3,)),
]
STEPS = NB + 3
GATHERED = 10
HALF = 7


def gate_grads(g, u, dh):
    s = jax.nn.sigmoid(g)
    sg = g * s
    hid = (sg * u).astype(BF16)
    dh = dh.astype(BF16).astype(F32)
    dgate = (dh * u * (s * (1.0 + g * (1.0 - s)))).astype(BF16)
    dup = (dh * sg).astype(BF16)
    return hid, dgate, dup


def weight_grads(ex, t, at_ref, dt_ref, hid_s, dg_s, du_s):
    slot = lax.rem(t, 2)
    store_pieces(ex.g, slot, 0, dot(at_ref[...], dg_s[...]))
    store_pieces(ex.g, slot, 1, dot(at_ref[...], du_s[...]))
    store_pieces(ex.g, slot, 2, dot(dt_ref[...], hid_s[...]).T)


def around(ex, gathered, e_refs, compute):
    t = pl.program_id(0)

    @pl.when(t == 0)
    def _():
        ex.greet()

    @pl.when(t >= 2)
    def _():
        ex.wait_peers()

    @pl.when(t < NB)
    def _():
        compute(t)
        for cp in ex.pair(t):
            cp.start()

    ex.stages(t, gathered, e_refs)
    ex.tell_peers()

    @pl.when(t == STEPS - 1)
    def _():
        ex.wait_peers(2)


def last_layer_kernel(a_ref, at_ref, dy_ref, dyt_ref, h_ref, wg_ref, wu_ref, wd_ref, e_ref, f_ref, dh_ref, acc, g_s, u_s, dh_s, hid_s, dg_s, du_s, *scratch):
    ex = Exchange(scratch, f_ref)

    def compute(t):
        @pl.when(t == 0)
        def _():
            acc[...] = jnp.zeros((T, D), F32)

        def front(rows):
            a = a_ref[rows, :]
            g_s[rows, :] = dot(a, wg_ref[0])
            u_s[rows, :] = dot(a, wu_ref[0])
            dh_s[rows, :] = dot_nt(dy_ref[rows, :], wd_ref[0])

        def back(rows):
            hid, dgate, dup = gate_grads(g_s[rows, :], u_s[rows, :], dh_s[rows, :])
            hid_s[rows, :] = hid
            dg_s[rows, :] = dgate
            du_s[rows, :] = dup
            acc[rows, :] += dot_nt(dgate, wg_ref[0]) + dot_nt(dup, wu_ref[0])

        pipelined(front, back)
        weight_grads(ex, t, at_ref, dyt_ref, hid_s, dg_s, du_s)

    around(ex, GATHERED, [(GATHERED, NB, e_ref)], compute)

    @pl.when(pl.program_id(0) == NB)
    def _():
        def chunk(i, _):
            rows = pl.ds(pl.multiple_of(i * CH, CH), CH)
            wide = h_ref[rows, :].astype(F32)
            da = acc[rows, :].astype(BF16).astype(F32)
            scale = lax.rsqrt(jnp.mean(wide * wide, -1, keepdims=True) + EPS)
            inner = jnp.mean(da * wide, -1, keepdims=True)
            back = (da * scale - wide * (scale * scale * scale * inner)).astype(BF16)
            dh_ref[rows, :] = (dy_ref[rows, :].astype(F32) + back.astype(F32)).astype(BF16)
            return 0

        lax.fori_loop(0, T // CH, chunk, 0)


def first_layer_kernel(at_ref, dh_ref, dht_ref, gate_ref, up_ref, wd_ref, ea_ref, eb_ref, dh_s, hid_s, dg_s, du_s, *scratch):
    ex = Exchange(scratch)

    def compute(t):
        def front(rows):
            dh_s[rows, :] = dot_nt(dh_ref[rows, :], wd_ref[0])

        def back(rows):
            hid, dgate, dup = gate_grads(gate_ref[rows, :], up_ref[rows, :], dh_s[rows, :])
            hid_s[rows, :] = hid
            dg_s[rows, :] = dgate
            du_s[rows, :] = dup

        pipelined(front, back)
        weight_grads(ex, t, at_ref, dht_ref, hid_s, dg_s, du_s)

    around(ex, 0, [(0, HALF, ea_ref), (HALF, NB, eb_ref)], compute)


def at_step(t):
    return jnp.minimum(t, NB - 1)


PIECES = (2, 3, 64, BLK)
FULL = (2, 2, 2, 2, 3, 64, BLK)


def sums_spec(begin, end):
    return pl.BlockSpec((1,) + PIECES, lambda t: (jnp.clip(t - 3 - begin, 0, end - begin - 1), 0, 0, 0, 0))


def sums_shape(begin, end):
    return jax.ShapeDtypeStruct((end - begin,) + PIECES, BF16)


HALVES = [pltpu.VMEM((T, BLK), BF16)] * 3


def last_layer(a, at, dy, dyt, h, wg, wu, wd):
    return pl.pallas_call(
        last_layer_kernel,
        grid=(STEPS,),
        in_specs=[
            whole((T, D)),
            whole((D, T)),
            whole((T, D)),
            whole((D, T)),
            whole((T, D)),
            pl.BlockSpec((1, D, BLK), lambda t: (1, 0, at_step(t))),
            pl.BlockSpec((1, D, BLK), lambda t: (1, 0, at_step(t))),
            pl.BlockSpec((1, BLK, D), lambda t: (1, at_step(t), 0)),
        ],
        out_specs=[sums_spec(GATHERED, NB), pl.BlockSpec(memory_space=pl.ANY), whole((T, D))],
        out_shape=[sums_shape(GATHERED, NB), jax.ShapeDtypeStruct((GATHERED,) + FULL, BF16), jax.ShapeDtypeStruct((T, D), BF16)],
        scratch_shapes=[pltpu.VMEM((T, D), F32), *[pltpu.VMEM((T, BLK), F32)] * 3, *HALVES, *EXCHANGE_SCRATCH],
        compiler_params=pltpu.CompilerParams(vmem_limit_bytes=VMEM_LIMIT, collective_id=0, has_side_effects=True),
        cost_estimate=pl.CostEstimate(flops=16 * T * D * FF, bytes_accessed=6 * D * FF, transcendentals=T * FF),
        name="last_layer",
    )(a, at, dy, dyt, h, wg, wu, wd)


def first_layer(at, dh, dht, gate, up, wd):
    return pl.pallas_call(
        first_layer_kernel,
        grid=(STEPS,),
        in_specs=[
            whole((D, T)),
            whole((T, D)),
            whole((D, T)),
            pl.BlockSpec((T, BLK), lambda t: (0, at_step(t))),
            pl.BlockSpec((T, BLK), lambda t: (0, at_step(t))),
            pl.BlockSpec((1, BLK, D), lambda t: (0, at_step(t), 0)),
        ],
        out_specs=[sums_spec(0, HALF), sums_spec(HALF, NB)],
        out_shape=[sums_shape(0, HALF), sums_shape(HALF, NB)],
        scratch_shapes=[pltpu.VMEM((T, BLK), F32), *HALVES, *EXCHANGE_SCRATCH],
        compiler_params=pltpu.CompilerParams(vmem_limit_bytes=VMEM_LIMIT, collective_id=1, has_side_effects=True),
        cost_estimate=pl.CostEstimate(flops=8 * T * D * FF, bytes_accessed=8 * T * FF, transcendentals=T * FF),
        name="first_layer",
    )(at, dh, dht, gate, up, wd)


def adamw(w, m, v, g):
    m = 0.9 * m + 0.1 * g
    v = 0.95 * v + 0.05 * g * g
    step = m * lax.rsqrt(v + 1e-8) + 0.1 * w
    return (w - 0.02 * step).astype(BF16), m, v


def adamw_kernel(own, g_ref, *refs):
    ins, outs = refs[:9], refs[-9:]
    for x, y, c, ab in itertools.product(range(2), repeat=4):
        d = x * 4 + y * 2 + c
        at = (d, 0, ab) if not own else (0, c, ab, x, y) if ab == 0 else (0, c, ab, y, x)
        for q in range(3):
            w_ref, m_ref, v_ref = ins[q], ins[3 + q], ins[6 + q]
            wo_ref, mo_ref, vo_ref = outs[q], outs[3 + q], outs[6 + q]
            if q < 2:
                parts = [(pl.ds(d * 128 + ab * 64, 64), slice(None), slice(None))]
            else:
                parts = [(pl.ds(d * 32 + ab * 16, 16), pl.ds(k * 256, 256), pl.ds(k * 16, 16)) for k in range(4)]
            for r, cols, of in parts:
                g = g_ref[(*at, q, of)].astype(F32)
                wo_ref[0, r, cols], mo_ref[0, r, cols], vo_ref[0, r, cols] = adamw(
                    w_ref[0, r, cols].astype(F32), m_ref[0, r, cols], v_ref[0, r, cols], g
                )


def update(layer, begin, g, arrays, before):
    own = g.ndim == 8
    count = g.shape[0] if own else g.shape[1]
    g_spec = pl.BlockSpec((1,) + FULL, lambda j: (j,) + (0,) * 7) if own else pl.BlockSpec((8, 1) + PIECES, lambda j: (0, j, 0, 0, 0, 0))
    wide = pl.BlockSpec((1, D, BLK), lambda j: (layer, 0, begin + j))
    tall = pl.BlockSpec((1, BLK, D), lambda j: (layer, begin + j, 0))
    specs = [wide, wide, tall] * 3
    held = [] if before is None else list(before)
    size = 3 * D * BLK * count
    return pl.pallas_call(
        functools.partial(adamw_kernel, own),
        grid=(count,),
        in_specs=[g_spec, *specs, *[pl.BlockSpec(memory_space=pl.ANY)] * len(held)],
        out_specs=specs,
        out_shape=[jax.ShapeDtypeStruct(a.shape, a.dtype) for a in arrays],
        input_output_aliases={10 + i: i for i in range(len(held))},
        compiler_params=pltpu.CompilerParams(vmem_limit_bytes=VMEM_LIMIT),
        cost_estimate=pl.CostEstimate(flops=30 * size, bytes_accessed=22 * size, transcendentals=size),
        name=f"adamw{layer}_{begin}",
    )(g, *arrays, *held)


def solution(mesh):
    def step(x, dy, wg, wu, wd, *moments):
        x, dy = x[0], dy[0]
        gate, up, h1, a1, a0t, dyt = forward(x, dy, wg, wu, wd)
        e1, f1, dh1 = last_layer(a1, a1.T, dy, dyt, h1, wg, wu, wd)
        g1 = lax.all_gather(e1, "dp", axis=0, tiled=False)
        e0a, e0b = first_layer(a0t, dh1, dh1.T, gate, up, wd)
        g0a = lax.all_gather(e0a, "dp", axis=0, tiled=False)
        g0b = lax.all_gather(e0b, "dp", axis=0, tiled=False)
        f1, e0a = lax.optimization_barrier((f1, e0a))
        arrays = (wg, wu, wd, *moments)
        new = update(1, 0, f1, arrays, None)
        new = update(1, GATHERED, g1, arrays, new)
        new = update(0, 0, g0a, arrays, new)
        return tuple(update(0, HALF, g0b, arrays, new))

    return jax.shard_map(
        step,
        mesh=mesh,
        in_specs=(P(("rep", "dp"), None, None),) * 2 + (P(None, None, None),) * 9,
        out_specs=(P("rep", None, None),) * 9,
        check_vma=False,
    )
```

time: 689 us -> 553 us (0.80)
  Pallas kernels: 613 us -> 525 us
  waiting for transfers between devices: 26.1 us -> 0.78 us
  local copies, waits for them, and re-layouts: 25.7 us -> 13.1 us
  other arithmetic: 8.64 us -> 0 us
    pallas_call x1, Pallas kernels: 236 us -> 193 us  [last_layer(): pl.pallas_call(last_layer_kernel, grid=(STEPS,), in_specs=[whole((T, D)),...]
    pallas_call x1, Pallas kernels: 166 us -> 124 us  [first_layer(): pl.pallas_call(first_layer_kernel, grid=(STEPS,), in_specs=[whole((D, T))...]
    all_gather x1 -> x2, waiting for transfers between devices: 26 us -> 0.04 us  [the longest x1 0.02 us: step(): g0a = lax.all_gather(e0a, 'dp', axis=0, tiled=False)]
    unnamed x2 -> x0, local copies, waits for them, and re-layouts: 12.9 us -> none
    pallas_call x2 -> x4, Pallas kernels: 148 us -> 149 us  [update(): pl.pallas_call(functools.partial(adamw_kernel, own), grid=(count,), in_sp...]
  transfers between devices with their start and end apart: 2 -> 3, of which waited for: 1 -> 0; matrix products, arithmetic and copies ran while one was open for 3% -> 1% of each run, Pallas kernels for 35% -> 44%
where the time goes in v2:
time: 553 us; the launch traced here: 552 us
  Pallas kernels  525 us (95%)
  between operations  13.8 us (2%)
  local copies, waits for them, and re-layouts  13.1 us (2%)
    pallas_call x1, Pallas kernels, last_layer(): pl.pallas_call(last_layer_kernel, grid=(STEPS,), in_specs=[whole((T, D)),...  193 us
    pallas_call x4, Pallas kernels, update(): pl.pallas_call(functools.partial(adamw_kernel, own), grid=(count,), in_sp...  149 us
    pallas_call x1, Pallas kernels, first_layer(): pl.pallas_call(first_layer_kernel, grid=(STEPS,), in_specs=[whole((D, T))...  124 us
    pallas_call x1, Pallas kernels, forward(): pl.pallas_call(forward_kernel, grid=(NB,), in_specs=[whole((T, D)), pl.Bl...  57.6 us
  transfers between devices with their start and end apart: 3, of which 0 were waited for; matrix products, arithmetic and copies ran while one was open for 1% of the time, Pallas kernels for 44%

profile of v2, /device:TPU:0, one launch (start us, length us, event | category | flops | bytes accessed | tf_op | source)
XLA Modules:
  0.0 552.3 jit_solution(14638465240193260749)
XLA Ops:
  7.2 0.0 all-gather.11.cloned.1.call-start
  7.2 57.6 %fwd0.1 = (f32[2048,3328]{1,0:T(8,128)}, f32[2048,3328]{1,0:T(8,128)}, bf16[2048,1024]{1,0:T(8,128)(2,1)}, bf16[2048,1024]{1,0:T(8,128)(2,1)}, bf16[1024,2048]{1,0:T(8,128)(2,1)}, /*index=5*/bf16[1024,2048]{1,0:T(8,128)(2,1)}) custom-call(bf16[2048,1024]{1,0:T(8,128)(2,1)} %bitcast.12, bf16[2048,1024]{1,0:T(8,128)(2,1)} %bitcast.13, ...), custom_call_target="tpu_custom_call" | custom-call | flops 41875931136 | bytes 54525952 | tf_op jit(solution)/shard_map/fwd0/pallas_call | solution.py:93
  64.8 6.4 %copy.49 = bf16[2048,1024]{0,1:T(8,128)(2,1)} copy(bf16[2048,1024]{1,0:T(8,128)(2,1)} %get-tuple-element.49.a_ref) | data formatting | bytes 8388608 | tf_op jit(solution)/shard_map/fwd0/pallas_call | solution.py:93
  71.3 193.2 %last_layer.1 = (bf16[3,2,3,64,256]{4,3,2,1,0:T(8,128)(2,1)}, bf16[10,2,2,2,2,3,64,256]{7,6,5,4,3,2,1,0:T(8,128)(2,1)}, bf16[2048,1024]{1,0:T(8,128)(2,1)}) custom-call(bf16[2048,1024]{1,0:T(8,128)(2,1)} %get-tuple-element.49.a_ref, bf16[1024,2048]{1,0:T(8,128)(2,1)} %bitcast.11, bf16[2048,1024]{1,0:T(8,128)(2,1)} %bitcast.14, ...), custom_call_target="tpu_custom_call" | custom-call | flops 111669149696 | bytes 20447232 | tf_op jit(solution)/shard_map/last_layer/pallas_call | solution.py:441
  264.4 0.0 all-gather.11.cloned.1.call-update
  264.4 0.0 all-gather.9.cloned.1.call-start
  264.5 6.7 %copy.50 = bf16[2048,1024]{0,1:T(8,128)(2,1)} copy(bf16[2048,1024]{1,0:T(8,128)(2,1)} %get-tuple-element.52.dh_ref) | data formatting | bytes 8388608 | tf_op jit(solution)/shard_map/last_layer/pallas_call | solution.py:441
  271.1 124.5 %first_layer.1 = (bf16[7,2,3,64,256]{4,3,2,1,0:T(8,128)(2,1)}, bf16[6,2,3,64,256]{4,3,2,1,0:T(8,128)(2,1)}) custom-call(bf16[1024,2048]{1,0:T(8,128)(2,1)} %get-tuple-element.48.at_ref, bf16[2048,1024]{1,0:T(8,128)(2,1)} %get-tuple-element.52.dh_ref, bf16[1024,2048]{1,0:T(8,128)(2,1)} %bitcast.10, f32[2048,3328]{1,0:T(8,128)} %get-tuple-element.53.gate_ref, ...), custom_call_target="tpu_custom_call" | custom-call | flops 55834574848 | bytes 54525952 | tf_op jit(solution)/shard_map/first_layer/pallas_call | solution.py:464
  395.6 0.0 all-gather.9.cloned.1.call-update
  395.7 0.0 all-gather.7.cloned.1.call-start
  395.7 0.7 all-gather.7.cloned.1.call-update
  396.4 54.9 %adamw1_0.1 = (bf16[2,1024,3328]{2,1,0:T(8,128)(2,1)}, bf16[2,1024,3328]{2,1,0:T(8,128)(2,1)}, bf16[2,3328,1024]{2,1,0:T(8,128)(2,1)}, f32[2,1024,3328]{2,1,0:T(...) custom-call(bf16[10,2,2,2,2,3,64,256]{7,6,5,4,3,2,1,0:T(8,128)(2,1)}, ...), custom_call_target="tpu_custom_call" | custom-call | flops 235929600 | bytes 173015040 | tf_op jit(solution)/shard_map/adamw1_0/pallas_call | solution.py:519
  451.3 0.0 all-gather.11.cloned.1.call-done
  451.3 19.8 %adamw1_10.1 = (bf16[2,1024,3328]{2,1,0:T(8,128)(2,1)}, bf16[2,1024,3328]{2,1,0:T(8,128)(2,1)}, bf16[2,3328,1024]{2,1,0:T(8,128)(2,1)}, f32[2,1024,3328]{2,1,0:T...) custom-call(bf16[8,3,2,3,64,256]{5,4,3,2,1,0:T(8,128)(2,1)} %bitcast, ...), custom_call_target="tpu_custom_call", output_to_operand_aliasing={{0}: (10, {}), {1}: (11, {}), {2}: (12, {}), {3}: (13, {}),... | custom-call | flops 70778880 | bytes 51904512 | tf_op jit(solution)/shard_map/adamw1_10/pallas_call | solution.py:519
  471.1 0.0 all-gather.9.cloned.1.call-done
  471.1 41.5 %adamw0_0.1 = (bf16[2,1024,3328]{2,1,0:T(8,128)(2,1)}, bf16[2,1024,3328]{2,1,0:T(8,128)(2,1)}, bf16[2,3328,1024]{2,1,0:T(8,128)(2,1)}, f32[2,1024,3328]{2,1,0:T(...) custom-call(bf16[8,7,2,3,64,256]{5,4,3,2,1,0:T(8,128)(2,1)} %bitcast, ...), custom_call_target="tpu_custom_call", output_to_operand_aliasing={{0}: (10, {}), {1}: (11, {}), {2}: (12, {}), {3}: (13, {}),... | custom-call | flops 165150720 | bytes 121110528 | tf_op jit(solution)/shard_map/adamw0_0/pallas_call | solution.py:519
  512.6 0.0 all-gather.7.cloned.1.call-done
  512.7 33.1 %adamw0_7.1 = (bf16[2,1024,3328]{2,1,0:T(8,128)(2,1)}, bf16[2,1024,3328]{2,1,0:T(8,128)(2,1)}, bf16[2,3328,1024]{2,1,0:T(8,128)(2,1)}, f32[2,1024,3328]{2,1,0:T(...) custom-call(bf16[8,6,2,3,64,256]{5,4,3,2,1,0:T(8,128)(2,1)} %bitcast, ...), custom_call_target="tpu_custom_call", output_to_operand_aliasing={{0}: (10, {}), {1}: (11, {}), {2}: (12, {}), {3}: (13, {}),... | custom-call | flops 141557760 | bytes 103809024 | tf_op jit(solution)/shard_map/adamw0_7/pallas_call | solution.py:519
Async XLA Ops:
  7.2 444.2 %all-gather.11.cloned.1.call-start = ((), (), s32[]{:S(2)}) async-start(), calls=%async_computation.2 | async-start | bytes 5308416 | tf_op jit(solution)/shard_map/all_gather | solution.py:537
  264.4 206.7 %all-gather.9.cloned.1.call-start = ((), (), s32[]{:S(2)}) async-start(), calls=%async_computation.1 | async-start | bytes 12386304 | tf_op jit(solution)/shard_map/all_gather | solution.py:539
  395.7 117.0 %all-gather.7.cloned.1.call-start = ((), (), s32[]{:S(2)}) async-start(), calls=%async_computation | async-start | bytes 10616832 | tf_op jit(solution)/shard_map/all_gather | solution.py:540
Sparse Core Ops, SparseCore 0:
  264.6 37.1 all-gather.10
  395.8 59.6 all-gather.8
  457.2 52.9 all-gather.6

commit v3 on v2

v3 whole, which is shorter than its diff:
```python
import functools
import itertools

import jax
import jax.numpy as jnp
from jax import lax
from jax.experimental import pallas as pl
from jax.experimental.pallas import tpu as pltpu
from jax.sharding import PartitionSpec as P

F32, BF16 = jnp.float32, jnp.bfloat16
T, D, FF = 2048, 1024, 3328
BLK = 256
NB = FF // BLK
CH = 512
TURN = 256
EPS = 1e-6
MESH = pl.DeviceIdType.MESH
VMEM_LIMIT = 64 * 1024 * 1024 - 65536 - 1024 * 1024


def dot(a, b):
    return lax.dot_general(a, b, (((1,), (0,)), ((), ())), preferred_element_type=F32)


def dot_nt(a, b):
    return lax.dot_general(a, b, (((1,), (1,)), ((), ())), preferred_element_type=F32)


def whole(shape):
    return pl.BlockSpec(shape, lambda *_: (0,) * len(shape), pipeline_mode=pl.Buffered(1))


def sigmoid(g):
    return 0.5 * jnp.tanh(0.5 * g) + 0.5


def norm_rows(h):
    wide = h.astype(F32)
    scale = lax.rsqrt(jnp.mean(wide * wide, -1, keepdims=True) + EPS)
    return (wide * scale).astype(BF16)


def turn_step(j):
    return jnp.minimum(j, T // TURN - 1)


def pipelined(front, back):
    chunks = [pl.ds(i * CH, CH) for i in range(T // CH)]
    front(chunks[0])
    for i, rows in enumerate(chunks):
        if i + 1 < len(chunks):
            front(chunks[i + 1])
        back(rows)


def by_gate_and_up(g, u):
    s = sigmoid(g)
    sg = g * s
    return (sg * u).astype(BF16), u * (s + sg * (1.0 - s)), sg


def forward_kernel(x_ref, dy_ref, wg_ref, wu_ref, wd_ref, by_gate_ref, by_up_ref, hid_ref, h_ref, a_ref, at_ref, dyt_ref, a0, acc, g_s, u_s):
    j = pl.program_id(0)

    @pl.when(j == 0)
    def _():
        def prepare(i, _):
            rows = pl.ds(pl.multiple_of(i * CH, CH), CH)
            a0[rows, :] = norm_rows(x_ref[rows, :])
            acc[rows, :] = jnp.zeros((CH, D), F32)
            return 0

        lax.fori_loop(0, T // CH, prepare, 0)

    def front(rows):
        a = a0[rows, :]
        by_gate_ref[rows, :] = dot(a, wg_ref[0])
        by_up_ref[rows, :] = dot(a, wu_ref[0])

    def back(rows):
        g = by_gate_ref[rows, :]
        hid = (g * sigmoid(g) * by_up_ref[rows, :]).astype(BF16)
        hid_ref[rows, :] = hid
        acc[rows, :] += dot(hid, wd_ref[0])

    at_ref[...] = a0[pl.ds(pl.multiple_of(turn_step(j) * TURN, TURN), TURN), :].T
    dyt_ref[...] = dy_ref[...].T
    pipelined(front, back)

    @pl.when(j == NB - 1)
    def _():
        def finish(i, _):
            rows = pl.ds(pl.multiple_of(i * CH, CH), CH)
            h = (x_ref[rows, :].astype(F32) + acc[rows, :].astype(BF16).astype(F32)).astype(BF16)
            h_ref[rows, :] = h
            a_ref[rows, :] = norm_rows(h)
            return 0

        lax.fori_loop(0, T // CH, finish, 0)


def forward(x, dy, wg, wu, wd):
    return pl.pallas_call(
        forward_kernel,
        grid=(NB,),
        in_specs=[
            whole((T, D)),
            pl.BlockSpec((TURN, D), lambda j: (turn_step(j), 0)),
            pl.BlockSpec((1, D, BLK), lambda j: (0, 0, j)),
            pl.BlockSpec((1, D, BLK), lambda j: (0, 0, j)),
            pl.BlockSpec((1, BLK, D), lambda j: (0, j, 0)),
        ],
        out_specs=[
            pl.BlockSpec((T, BLK), lambda j: (0, j)),
            pl.BlockSpec((T, BLK), lambda j: (0, j)),
            pl.BlockSpec((T, BLK), lambda j: (0, j)),
            whole((T, D)),
            whole((T, D)),
            pl.BlockSpec((D, TURN), lambda j: (0, turn_step(j))),
            pl.BlockSpec((D, TURN), lambda j: (0, turn_step(j))),
        ],
        out_shape=[
            jax.ShapeDtypeStruct((T, FF), F32),
            jax.ShapeDtypeStruct((T, FF), F32),
            jax.ShapeDtypeStruct((T, FF), BF16),
            jax.ShapeDtypeStruct((T, D), BF16),
            jax.ShapeDtypeStruct((T, D), BF16),
            jax.ShapeDtypeStruct((D, T), BF16),
            jax.ShapeDtypeStruct((D, T), BF16),
        ],
        scratch_shapes=[pltpu.VMEM((T, D), BF16), pltpu.VMEM((T, D), F32), *[pltpu.VMEM((T, BLK), F32)] * 2],
        compiler_params=pltpu.CompilerParams(vmem_limit_bytes=VMEM_LIMIT),
        cost_estimate=pl.CostEstimate(flops=6 * T * D * FF, bytes_accessed=8 * T * FF, transcendentals=T * FF),
        name="fwd0",
    )(x, dy, wg, wu, wd)


SLOTS = 4
PAIR, FIRST, SECOND, BACK1, BACK2, BACK3 = 1, 2, 3, 4, 5, 6


def store_pieces(g_buf, slot, q, value):
    value = value.astype(BF16)
    for c in range(2):
        for ab in range(2):
            for s1 in range(2):
                for s2 in range(2):
                    x, y = (s1, s2) if ab == 0 else (s2, s1)
                    d = x * 4 + y * 2 + c
                    if q < 2:
                        r = d * 128 + ab * 64
                        g_buf[slot, c, ab, s1, s2, q] = value[r : r + 64]
                    else:
                        r = d * 32 + ab * 16
                        for k in range(4):
                            g_buf[slot, c, ab, s1, s2, q, k * 16 : k * 16 + 16] = value[r : r + 16, k * 256 : k * 256 + 256]


class Exchange:
    def __init__(self, scratch, f=None):
        self.g, self.h, self.q, self.e, self.r0, self.r1, self.r2 = scratch[:7]
        self.send, self.recv, self.keep, self.ahead = scratch[7:]
        self.f = f
        me = lax.axis_index("dp")
        self.rep = lax.axis_index("rep")
        self.x, self.y, self.c = me // 4, (me // 2) % 2, me % 2
        self.nx = (1 - self.x) * 4 + self.y * 2 + self.c
        self.ny = self.x * 4 + (1 - self.y) * 2 + self.c
        self.nc = self.x * 4 + self.y * 2 + (1 - self.c)

    def copy(self, kind, block, src, dst, to):
        slot = lax.rem(block, SLOTS)
        return pltpu.make_async_remote_copy(
            src_ref=src,
            dst_ref=dst,
            send_sem=self.send.at[kind, slot],
            recv_sem=self.recv.at[kind, slot],
            device_id=(self.rep, to),
            device_id_type=MESH,
        )

    def pair(self, b):
        return [self.copy(0, b, self.g.at[lax.rem(b, 2), 1 - self.c], self.r0.at[lax.rem(b, SLOTS)], self.nc)]

    def first(self, b):
        s, p = lax.rem(b, SLOTS), lax.rem(b, 2)
        return [
            self.copy(1, b, self.h.at[p, 0, 1 - self.x], self.r1.at[s, 0], self.nx),
            self.copy(2, b, self.h.at[p, 1, 1 - self.y], self.r1.at[s, 1], self.ny),
        ]

    def second(self, b):
        s, p = lax.rem(b, SLOTS), lax.rem(b, 2)
        return [
            self.copy(3, b, self.q.at[p, 0, 1 - self.y], self.r2.at[s, 0], self.ny),
            self.copy(4, b, self.q.at[p, 1, 1 - self.x], self.r2.at[s, 1], self.nx),
        ]

    def greet(self):
        barrier = pltpu.get_barrier_semaphore()
        for n in (self.nx, self.ny, self.nc):
            pl.semaphore_signal(barrier, inc=1, device_id=(self.rep, n), device_id_type=MESH)
        pl.semaphore_wait(barrier, 3)

    def wait_peers(self, count=1):
        for k in range(3):
            pl.semaphore_wait(self.ahead.at[k], count)

    def tell_peers(self):
        for k, n in enumerate((self.nx, self.ny, self.nc)):
            pl.semaphore_signal(self.ahead.at[k], inc=1, device_id=(self.rep, n), device_id_type=MESH)

    def mine(self, ab):
        return (self.x, self.y) if ab == 0 else (self.y, self.x)

    def own(self, b):
        return [pltpu.make_async_copy(self.e.at[lax.rem(b, SLOTS), ab], self.f.at[(b, self.c, ab, *self.mine(ab))], self.keep.at[lax.rem(b, SLOTS), ab]) for ab in range(2)]

    def back_first(self, b):
        return [self.copy(5 + ab, b, self.e.at[lax.rem(b, SLOTS), ab], self.f.at[(b, self.c, ab, *self.mine(ab))], (self.ny, self.nx)[ab]) for ab in range(2)]

    def back_second(self, b):
        out = []
        for ab in range(2):
            part = self.f.at[b, self.c, ab, self.mine(ab)[0]]
            out.append(self.copy(7 + ab, b, part, part, (self.nx, self.ny)[ab]))
        return out

    def back_pair(self, b):
        return [self.copy(9, b, self.f.at[b, self.c], self.f.at[b, self.c], self.nc)]

    def sums(self, b, out):
        s = lax.rem(b, SLOTS)
        for ab in range(2):
            s2 = self.mine(ab)[1]
            out[ab] = (self.q[lax.rem(b, 2), ab, s2].astype(F32) + self.r2[s, ab].astype(F32)).astype(BF16)

    def stages(self, t, gathered, e_refs):
        def at(lag, end, begin=0):
            return (t >= begin + lag) & (t < end + lag)

        @pl.when(at(PAIR, ALL))
        def _():
            b = t - PAIR
            s = lax.rem(b, SLOTS)
            g = lax.rem(b, 2)
            for cp in self.pair(b):
                cp.wait()

            def add(k, _):
                ab, s1, s2 = k // 4, (k // 2) % 2, k % 2
                self.h[g, ab, s1, s2] = (self.g[g, self.c, ab, s1, s2].astype(F32) + self.r0[s, ab, s1, s2].astype(F32)).astype(BF16)
                return 0

            lax.fori_loop(0, 8, add, 0)
            for cp in self.first(b):
                cp.start()

        @pl.when(at(FIRST, ALL))
        def _():
            b = t - FIRST
            s, p = lax.rem(b, SLOTS), lax.rem(b, 2)
            for cp in self.first(b):
                cp.wait()
            for ab in range(2):
                s1 = self.mine(ab)[0]
                for s2 in range(2):
                    self.q[p, ab, s2] = (self.h[p, ab, s1, s2].astype(F32) + self.r1[s, ab, s2].astype(F32)).astype(BF16)
            for cp in self.second(b):
                cp.start()

        @pl.when(at(SECOND, ALL))
        def _():
            for cp in self.second(t - SECOND):
                cp.wait()

        if gathered:

            @pl.when(at(SECOND, gathered))
            def _():
                b = t - SECOND
                self.sums(b, self.e.at[lax.rem(b, SLOTS)])
                for cp in self.own(b) + self.back_first(b):
                    cp.start()

        for begin, end, e_ref in e_refs:

            @pl.when(at(SECOND, end, begin))
            def _(e_ref=e_ref):
                self.sums(t - SECOND, e_ref.at[0])

        if gathered:

            @pl.when(at(BACK1, gathered))
            def _():
                for cp in self.own(t - BACK1) + self.back_first(t - BACK1):
                    cp.wait()
                for cp in self.back_second(t - BACK1):
                    cp.start()

            @pl.when(at(BACK2, gathered))
            def _():
                for cp in self.back_second(t - BACK2):
                    cp.wait()
                for cp in self.back_pair(t - BACK2):
                    cp.start()

            @pl.when(at(BACK3, gathered))
            def _():
                for cp in self.back_pair(t - BACK3):
                    cp.wait()


EXCHANGE_SCRATCH = [
    pltpu.VMEM((2, 2, 2, 2, 2, 3, 64, BLK), BF16),
    pltpu.VMEM((2, 2, 2, 2, 3, 64, BLK), BF16),
    pltpu.VMEM((2, 2, 2, 3, 64, BLK), BF16),
    pltpu.VMEM((SLOTS, 2, 3, 64, BLK), BF16),
    pltpu.VMEM((SLOTS, 2, 2, 2, 3, 64, BLK), BF16),
    pltpu.VMEM((SLOTS, 2, 2, 3, 64, BLK), BF16),
    pltpu.VMEM((SLOTS, 2, 3, 64, BLK), BF16),
    pltpu.SemaphoreType.DMA((10, SLOTS)),
    pltpu.SemaphoreType.DMA((10, SLOTS)),
    pltpu.SemaphoreType.DMA((SLOTS, 2)),
    pltpu.SemaphoreType.REGULAR((3,)),
]
ALL = 2 * NB
STEPS = ALL + SECOND
HALF = 7


def weight_grads(ex, t, at_ref, dt_ref, hid_s, dg_s, du_s):
    slot = lax.rem(t, 2)
    store_pieces(ex.g, slot, 0, dot(at_ref[...], dg_s[...]))
    store_pieces(ex.g, slot, 1, dot(at_ref[...], du_s[...]))
    store_pieces(ex.g, slot, 2, dot(dt_ref[...], hid_s[slot]).T)


def backward_kernel(
    a_hbm, dy_hbm, dyt_hbm, h_hbm, a0t_hbm, by_gate_hbm, by_up_hbm, hid_hbm, wg_ref, wu_ref, wd_ref,
    e0a_ref, e0b_ref, f_ref,
    a_s, at_s, d_s, dt_s, acc, g_s, u_s, dh_s, hid_s, dg_s, du_s, loads, *scratch,
):
    ex = Exchange(scratch, f_ref)
    t = pl.program_id(0)

    def load(k, src, dst):
        return pltpu.make_async_copy(src, dst, loads.at[k])

    def load_hidden(step):
        cols = pl.ds(pl.multiple_of((step - NB) * BLK, BLK), BLK)
        return [load(6, by_gate_hbm.at[:, cols], g_s), load(7, by_up_hbm.at[:, cols], u_s)]

    def load_units(step):
        cols = pl.ds(pl.multiple_of((step - NB) * BLK, BLK), BLK)
        return load(8 + lax.rem(step, 2), hid_hbm.at[:, cols], hid_s.at[lax.rem(step, 2)])

    load_a = load(0, a_hbm, a_s)
    other_loads = [load(1, dy_hbm, d_s), load(3, dyt_hbm, dt_s)]
    load_h = load(4, h_hbm, a_s)
    load_a0t = load(5, a0t_hbm, at_s)

    @pl.when(t == 0)
    def _():
        load_a.start()
        for cp in other_loads:
            cp.start()
        ex.greet()
        load_a.wait()

        def chunk(i, _):
            rows = pl.ds(pl.multiple_of(i * TURN, TURN), TURN)
            acc[rows, :] = jnp.zeros((TURN, D), F32)
            at_s[:, rows] = a_s[rows, :].T
            return 0

        lax.fori_loop(0, T // TURN, chunk, 0)
        for cp in other_loads:
            cp.wait()

    @pl.when(t >= 2)
    def _():
        ex.wait_peers()

    @pl.when((t >= NB - 1) & (t < ALL - 1))
    def _():
        load_units(t + 1).start()

    @pl.when(t < NB)
    def _():
        def front(rows):
            a = a_s[rows, :]
            g_s[rows, :] = dot(a, wg_ref[0])
            u_s[rows, :] = dot(a, wu_ref[0])
            dh_s[rows, :] = dot_nt(d_s[rows, :], wd_ref[0])

        def back(rows):
            hid_s[lax.rem(t, 2), rows, :], by_gate, by_up = by_gate_and_up(g_s[rows, :], u_s[rows, :])
            dh = dh_s[rows, :].astype(BF16).astype(F32)
            dgate = (dh * by_gate).astype(BF16)
            dup = (dh * by_up).astype(BF16)
            dg_s[rows, :] = dgate
            du_s[rows, :] = dup
            acc[rows, :] += dot_nt(dgate, wg_ref[0]) + dot_nt(dup, wu_ref[0])

        pipelined(front, back)
        weight_grads(ex, t, at_s, dt_s, hid_s, dg_s, du_s)

    @pl.when(t == NB - 1)
    def _():
        load_h.start()
        load_a0t.start()
        for cp in load_hidden(t + 1):
            cp.start()

    @pl.when(t == NB)
    def _():
        load_h.wait()

        def chunk(i, _):
            rows = pl.ds(pl.multiple_of(i * 256, 256), 256)
            wide = a_s[rows, :].astype(F32)
            da = acc[rows, :].astype(BF16).astype(F32)
            scale = lax.rsqrt(jnp.mean(wide * wide, -1, keepdims=True) + EPS)
            inner = jnp.mean(da * wide, -1, keepdims=True)
            back = (da * scale - wide * (scale * scale * scale * inner)).astype(BF16)
            dh = (d_s[rows, :].astype(F32) + back.astype(F32)).astype(BF16)
            d_s[rows, :] = dh
            dt_s[:, rows] = dh.T
            return 0

        lax.fori_loop(0, T // 256, chunk, 0)
        load_a0t.wait()

    @pl.when((t >= NB) & (t < ALL))
    def _():
        for cp in [*load_hidden(t), load_units(t)]:
            cp.wait()

        def front(rows):
            dh_s[rows, :] = dot_nt(d_s[rows, :], wd_ref[0])

        def back(rows):
            dh = dh_s[rows, :].astype(BF16).astype(F32)
            _, by_gate, by_up = by_gate_and_up(g_s[rows, :], u_s[rows, :])
            dg_s[rows, :] = (dh * by_gate).astype(BF16)
            du_s[rows, :] = (dh * by_up).astype(BF16)

        pipelined(front, back)

        @pl.when(t < ALL - 1)
        def _():
            for cp in load_hidden(t + 1):
                cp.start()

        weight_grads(ex, t, at_s, dt_s, hid_s, dg_s, du_s)

    @pl.when(t < ALL)
    def _():
        for cp in ex.pair(t):
            cp.start()

    ex.stages(t, NB, [(NB, NB + HALF, e0a_ref), (NB + HALF, ALL, e0b_ref)])
    ex.tell_peers()

    @pl.when(t == STEPS - 1)
    def _():
        ex.wait_peers(2)


PIECES = (2, 3, 64, BLK)
FULL = (2, 2, 2, 2, 3, 64, BLK)


def sums_spec(begin, end):
    return pl.BlockSpec((1,) + PIECES, lambda t: (jnp.clip(t - SECOND - begin, 0, end - begin - 1), 0, 0, 0, 0))


def sums_shape(begin, end):
    return jax.ShapeDtypeStruct((end - begin,) + PIECES, BF16)


def backward(a, dy, dyt, h, a0t, by_gate, by_up, hid, wg, wu, wd):
    any_spec = pl.BlockSpec(memory_space=pl.ANY)
    wide = pl.BlockSpec((1, D, BLK), lambda t: (1, 0, jnp.minimum(t, NB - 1)))
    tall = pl.BlockSpec((1, BLK, D), lambda t: (jnp.where(t < NB, 1, 0), jnp.where(t < NB, t, jnp.minimum(t, ALL - 1) - NB), 0))
    ends = [(NB, NB + HALF), (NB + HALF, ALL)]
    return pl.pallas_call(
        backward_kernel,
        grid=(STEPS,),
        in_specs=[any_spec] * 8 + [wide, wide, tall],
        out_specs=[*[sums_spec(*e) for e in ends], any_spec],
        out_shape=[*[sums_shape(*e) for e in ends], jax.ShapeDtypeStruct((NB,) + FULL, BF16)],
        scratch_shapes=[
            pltpu.VMEM((T, D), BF16),
            pltpu.VMEM((D, T), BF16),
            pltpu.VMEM((T, D), BF16),
            pltpu.VMEM((D, T), BF16),
            pltpu.VMEM((T, D), F32),
            *[pltpu.VMEM((T, BLK), F32)] * 3,
            pltpu.VMEM((2, T, BLK), BF16),
            *[pltpu.VMEM((T, BLK), BF16)] * 2,
            pltpu.SemaphoreType.DMA((10,)),
            *EXCHANGE_SCRATCH,
        ],
        compiler_params=pltpu.CompilerParams(vmem_limit_bytes=VMEM_LIMIT, collective_id=0, has_side_effects=True),
        cost_estimate=pl.CostEstimate(flops=24 * T * D * FF, bytes_accessed=12 * T * FF, transcendentals=2 * T * FF),
        name="backward",
    )(a, dy, dyt, h, a0t, by_gate, by_up, hid, wg, wu, wd)


def adamw(w, m, v, g):
    m = 0.9 * m + 0.1 * g
    v = 0.95 * v + 0.05 * g * g
    step = m * lax.rsqrt(v + 1e-8) + 0.1 * w
    return (w - 0.02 * step).astype(BF16), m, v


def adamw_kernel(own, g_ref, *refs):
    ins, outs = refs[:9], refs[-9:]
    for x, y, c, ab in itertools.product(range(2), repeat=4):
        d = x * 4 + y * 2 + c
        at = (d, 0, ab) if not own else (0, c, ab, x, y) if ab == 0 else (0, c, ab, y, x)
        for q in range(3):
            w_ref, m_ref, v_ref = ins[q], ins[3 + q], ins[6 + q]
            wo_ref, mo_ref, vo_ref = outs[q], outs[3 + q], outs[6 + q]
            if q < 2:
                parts = [(pl.ds(d * 128 + ab * 64, 64), slice(None), slice(None))]
            else:
                parts = [(pl.ds(d * 32 + ab * 16, 16), pl.ds(k * 256, 256), pl.ds(k * 16, 16)) for k in range(4)]
            for r, cols, of in parts:
                g = g_ref[(*at, q, of)].astype(F32)
                wo_ref[0, r, cols], mo_ref[0, r, cols], vo_ref[0, r, cols] = adamw(
                    w_ref[0, r, cols].astype(F32), m_ref[0, r, cols], v_ref[0, r, cols], g
                )


def update(layer, begin, g, arrays, before):
    own = g.ndim == 8
    count = g.shape[0] if own else g.shape[1]
    g_spec = pl.BlockSpec((1,) + FULL, lambda j: (j,) + (0,) * 7) if own else pl.BlockSpec((8, 1) + PIECES, lambda j: (0, j, 0, 0, 0, 0))
    wide = pl.BlockSpec((1, D, BLK), lambda j: (layer, 0, begin + j))
    tall = pl.BlockSpec((1, BLK, D), lambda j: (layer, begin + j, 0))
    specs = [wide, wide, tall] * 3
    held = [] if before is None else list(before)
    size = 3 * D * BLK * count
    return pl.pallas_call(
        functools.partial(adamw_kernel, own),
        grid=(count,),
        in_specs=[g_spec, *specs, *[pl.BlockSpec(memory_space=pl.ANY)] * len(held)],
        out_specs=specs,
        out_shape=[jax.ShapeDtypeStruct(a.shape, a.dtype) for a in arrays],
        input_output_aliases={10 + i: i for i in range(len(held))},
        compiler_params=pltpu.CompilerParams(vmem_limit_bytes=VMEM_LIMIT),
        cost_estimate=pl.CostEstimate(flops=30 * size, bytes_accessed=22 * size, transcendentals=size),
        name=f"adamw{layer}_{begin}",
    )(g, *arrays, *held)


def solution(mesh):
    def step(x, dy, wg, wu, wd, *moments):
        x, dy = x[0], dy[0]
        by_gate, by_up, hid, h1, a1, a0t, dyt = forward(x, dy, wg, wu, wd)
        e0a, e0b, f1 = backward(a1, dy, dyt, h1, a0t, by_gate, by_up, hid, wg, wu, wd)
        g0a, g0b = (lax.all_gather(e, "dp", axis=0, tiled=False) for e in (e0a, e0b))
        arrays = (wg, wu, wd, *moments)
        new = update(1, 0, f1, arrays, None)
        new = update(0, 0, g0a, arrays, new)
        return tuple(update(0, HALF, g0b, arrays, new))

    return jax.shard_map(
        step,
        mesh=mesh,
        in_specs=(P(("rep", "dp"), None, None),) * 2 + (P(None, None, None),) * 9,
        out_specs=(P("rep", None, None),) * 9,
        check_vma=False,
    )
```

time: 553 us -> 515 us (0.931)
  Pallas kernels: 525 us -> 500 us
  local copies, waits for them, and re-layouts: 13.1 us -> 0 us
    pallas_call x2 -> x1, Pallas kernels: 318 us -> 291 us  [backward(): pl.pallas_call(backward_kernel, grid=(STEPS,), in_specs=[any_spec] * 8 +...]
    pallas_call x2 -> x0, local copies, waits for them, and re-layouts: 13.1 us -> none  [the longest x1 6.65 us: last_layer(): pl.pallas_call(last_layer_kernel, grid=(STEPS,), in_specs=[whole((T, D)),...]
    pallas_call x4 -> x3, Pallas kernels: 149 us -> 149 us  [update(): pl.pallas_call(functools.partial(adamw_kernel, own), grid=(count,), in_sp...]
  transfers between devices with their start and end apart: 3 -> 2, of which waited for: 0 -> 0; matrix products, arithmetic and copies ran while one was open for 1% -> 0% of each run, Pallas kernels for 44% -> 22%
where the time goes in v3:
time: 515 us
  Pallas kernels  500 us (97%)
  between operations  14.1 us (3%)
    pallas_call x1, Pallas kernels, backward(): pl.pallas_call(backward_kernel, grid=(STEPS,), in_specs=[any_spec] * 8 +...  291 us
    pallas_call x3, Pallas kernels, update(): pl.pallas_call(functools.partial(adamw_kernel, own), grid=(count,), in_sp...  149 us
    pallas_call x1, Pallas kernels, forward(): pl.pallas_call(forward_kernel, grid=(NB,), in_specs=[whole((T, D)), pl.Bl...  60 us
  transfers between devices with their start and end apart: 2, of which 0 were waited for; matrix products, arithmetic and copies ran while one was open for 0% of the time, Pallas kernels for 22%

profile of v3, /device:TPU:0, one launch (start us, length us, event | category | flops | bytes accessed | tf_op | source)
XLA Modules:
  0.0 514.6 jit_solution(15050043288072957158)
XLA Ops:
  7.2 0.0 all-gather.7.cloned.1.call-start
  7.2 60.0 %fwd0.1 = (f32[2048,3328]{1,0:T(8,128)}, f32[2048,3328]{1,0:T(8,128)}, bf16[2048,3328]{1,0:T(8,128)(2,1)}, bf16[2048,1024]{1,0:T(8,128)(2,1)}, bf16[2048,1024]{1...) custom-call(bf16[2048,1024]{1,0:T(8,128)(2,1)} %bitcast.6, bf16[2048,1024]{1,0:T(8,128)(2,1)} %bitcast.7, ...), custom_call_target="tpu_custom_call" | custom-call | flops 41875931136 | bytes 54525952 | tf_op jit(solution)/shard_map/fwd0/pallas_call | solution.py:104
  67.2 290.9 %backward.1 = (bf16[7,2,3,64,256]{4,3,2,1,0:T(8,128)(2,1)}, bf16[6,2,3,64,256]{4,3,2,1,0:T(8,128)(2,1)}, bf16[13,2,2,2,2,3,64,256]{7,6,5,4,3,2,1,0:T(8,128)(2,1)}) custom-call(bf16[2048,1024]{1,0:T(8,128)(2,1)} %get-tuple-element.37.a_hbm, bf16[2048,1024]{1,0:T(8,128)(2,1)} %bitcast.8, bf16[1024,2048]{1,0:T(8,128)(2,1)} %get-tuple-element.38.dyt_hbm, ...), custom_call_target="tpu_custom_call" | custom-call | flops 167503724544 | bytes 81788928 | tf_op jit(solution)/shard_map/backward/pallas_call | solution.py:489
  358.1 0.0 all-gather.7.cloned.1.call-update
  358.1 0.0 all-gather.5.cloned.1.call-start
  358.2 0.7 all-gather.5.cloned.1.call-update
  358.9 74.2 %adamw1_0.1 = (bf16[2,1024,3328]{2,1,0:T(8,128)(2,1)}, bf16[2,1024,3328]{2,1,0:T(8,128)(2,1)}, bf16[2,3328,1024]{2,1,0:T(8,128)(2,1)}, f32[2,1024,3328]{2,1,0:T(...) custom-call(bf16[13,2,2,2,2,3,64,256]{7,6,5,4,3,2,1,0:T(8,128)(2,1)}, ...), custom_call_target="tpu_custom_call" | custom-call | flops 306708480 | bytes 224919552 | tf_op jit(solution)/shard_map/adamw1_0/pallas_call | solution.py:548
  433.1 0.0 all-gather.7.cloned.1.call-done
  433.1 41.5 %adamw0_0.1 = (bf16[2,1024,3328]{2,1,0:T(8,128)(2,1)}, bf16[2,1024,3328]{2,1,0:T(8,128)(2,1)}, bf16[2,3328,1024]{2,1,0:T(8,128)(2,1)}, f32[2,1024,3328]{2,1,0:T(...) custom-call(bf16[8,7,2,3,64,256]{5,4,3,2,1,0:T(8,128)(2,1)} %bitcast, ...), custom_call_target="tpu_custom_call", output_to_operand_aliasing={{0}: (10, {}), {1}: (11, {}), {2}: (12, {}), {3}: (13, {}),... | custom-call | flops 165150720 | bytes 121110528 | tf_op jit(solution)/shard_map/adamw0_0/pallas_call | solution.py:548
  474.6 0.0 all-gather.5.cloned.1.call-done
  474.7 33.1 %adamw0_7.1 = (bf16[2,1024,3328]{2,1,0:T(8,128)(2,1)}, bf16[2,1024,3328]{2,1,0:T(8,128)(2,1)}, bf16[2,3328,1024]{2,1,0:T(8,128)(2,1)}, f32[2,1024,3328]{2,1,0:T(...) custom-call(bf16[8,6,2,3,64,256]{5,4,3,2,1,0:T(8,128)(2,1)} %bitcast, ...), custom_call_target="tpu_custom_call", output_to_operand_aliasing={{0}: (10, {}), {1}: (11, {}), {2}: (12, {}), {3}: (13, {}),... | custom-call | flops 141557760 | bytes 103809024 | tf_op jit(solution)/shard_map/adamw0_7/pallas_call | solution.py:548
Async XLA Ops:
  7.2 425.9 %all-gather.7.cloned.1.call-start = ((), (), s32[]{:S(2)}) async-start(), calls=%async_computation.1 | async-start | bytes 12386304 | tf_op jit(solution)/shard_map/all_gather | solution.py:566
  358.1 116.5 %all-gather.5.cloned.1.call-start = ((), (), s32[]{:S(2)}) async-start(), calls=%async_computation | async-start | bytes 10616832 | tf_op jit(solution)/shard_map/all_gather | solution.py:566
Sparse Core Ops, SparseCore 0:
  358.2 60.1 all-gather.6
  420.2 52.9 all-gather.4

commit v4 on v3

--- a/solution.py
+++ b/solution.py
@@ -60,7 +60,7 @@
     return (sg * u).astype(BF16), u * (s + sg * (1.0 - s)), sg
 
 
-def forward_kernel(x_ref, dy_ref, wg_ref, wu_ref, wd_ref, by_gate_ref, by_up_ref, hid_ref, h_ref, a_ref, at_ref, dyt_ref, a0, acc, g_s, u_s):
+def forward_kernel(x_ref, dy_ref, wg_ref, wu_ref, wd_ref, gate_ref, up_ref, h_ref, a_ref, at_ref, dyt_ref, a0, acc, g_s, u_s):
     j = pl.program_id(0)
 
     @pl.when(j == 0)
@@ -75,13 +75,12 @@
 
     def front(rows):
         a = a0[rows, :]
-        by_gate_ref[rows, :] = dot(a, wg_ref[0])
-        by_up_ref[rows, :] = dot(a, wu_ref[0])
+        gate_ref[rows, :] = dot(a, wg_ref[0])
+        up_ref[rows, :] = dot(a, wu_ref[0])
 
     def back(rows):
-        g = by_gate_ref[rows, :]
-        hid = (g * sigmoid(g) * by_up_ref[rows, :]).astype(BF16)
-        hid_ref[rows, :] = hid
+        g = gate_ref[rows, :]
+        hid = (g * sigmoid(g) * up_ref[rows, :]).astype(BF16)
         acc[rows, :] += dot(hid, wd_ref[0])
 
     at_ref[...] = a0[pl.ds(pl.multiple_of(turn_step(j) * TURN, TURN), TURN), :].T
@@ -114,7 +113,6 @@
         out_specs=[
             pl.BlockSpec((T, BLK), lambda j: (0, j)),
             pl.BlockSpec((T, BLK), lambda j: (0, j)),
-            pl.BlockSpec((T, BLK), lambda j: (0, j)),
             whole((T, D)),
             whole((T, D)),
             pl.BlockSpec((D, TURN), lambda j: (0, turn_step(j))),
@@ -123,7 +121,6 @@
         out_shape=[
             jax.ShapeDtypeStruct((T, FF), F32),
             jax.ShapeDtypeStruct((T, FF), F32),
-            jax.ShapeDtypeStruct((T, FF), BF16),
             jax.ShapeDtypeStruct((T, D), BF16),
             jax.ShapeDtypeStruct((T, D), BF16),
             jax.ShapeDtypeStruct((D, T), BF16),
@@ -138,6 +135,7 @@
 
 SLOTS = 4
 PAIR, FIRST, SECOND, BACK1, BACK2, BACK3 = 1, 2, 3, 4, 5, 6
+FIRST_LATE, SECOND_LATE = 3, 5
 
 
 def store_pieces(g_buf, slot, q, value):
@@ -184,17 +182,17 @@
         return [self.copy(0, b, self.g.at[lax.rem(b, 2), 1 - self.c], self.r0.at[lax.rem(b, SLOTS)], self.nc)]
 
     def first(self, b):
-        s, p = lax.rem(b, SLOTS), lax.rem(b, 2)
+        s = lax.rem(b, SLOTS)
         return [
-            self.copy(1, b, self.h.at[p, 0, 1 - self.x], self.r1.at[s, 0], self.nx),
-            self.copy(2, b, self.h.at[p, 1, 1 - self.y], self.r1.at[s, 1], self.ny),
+            self.copy(1, b, self.h.at[s, 0, 1 - self.x], self.r1.at[s, 0], self.nx),
+            self.copy(2, b, self.h.at[s, 1, 1 - self.y], self.r1.at[s, 1], self.ny),
         ]
 
     def second(self, b):
-        s, p = lax.rem(b, SLOTS), lax.rem(b, 2)
+        s = lax.rem(b, SLOTS)
         return [
-            self.copy(3, b, self.q.at[p, 0, 1 - self.y], self.r2.at[s, 0], self.ny),
-            self.copy(4, b, self.q.at[p, 1, 1 - self.x], self.r2.at[s, 1], self.nx),
+            self.copy(3, b, self.q.at[s, 0, 1 - self.y], self.r2.at[s, 0], self.ny),
+            self.copy(4, b, self.q.at[s, 1, 1 - self.x], self.r2.at[s, 1], self.nx),
         ]
 
     def greet(self):
@@ -234,7 +232,7 @@
         s = lax.rem(b, SLOTS)
         for ab in range(2):
             s2 = self.mine(ab)[1]
-            out[ab] = (self.q[lax.rem(b, 2), ab, s2].astype(F32) + self.r2[s, ab].astype(F32)).astype(BF16)
+            out[ab] = (self.q[s, ab, s2].astype(F32) + self.r2[s, ab].astype(F32)).astype(BF16)
 
     def stages(self, t, gathered, e_refs):
         def at(lag, end, begin=0):
@@ -250,45 +248,49 @@
 
             def add(k, _):
                 ab, s1, s2 = k // 4, (k // 2) % 2, k % 2
-                self.h[g, ab, s1, s2] = (self.g[g, self.c, ab, s1, s2].astype(F32) + self.r0[s, ab, s1, s2].astype(F32)).astype(BF16)
+                self.h[s, ab, s1, s2] = (self.g[g, self.c, ab, s1, s2].astype(F32) + self.r0[s, ab, s1, s2].astype(F32)).astype(BF16)
                 return 0
 
             lax.fori_loop(0, 8, add, 0)
             for cp in self.first(b):
                 cp.start()
 
-        @pl.when(at(FIRST, ALL))
-        def _():
-            b = t - FIRST
-            s, p = lax.rem(b, SLOTS), lax.rem(b, 2)
+        def first_stage(b):
+            s = lax.rem(b, SLOTS)
             for cp in self.first(b):
                 cp.wait()
             for ab in range(2):
                 s1 = self.mine(ab)[0]
                 for s2 in range(2):
-                    self.q[p, ab, s2] = (self.h[p, ab, s1, s2].astype(F32) + self.r1[s, ab, s2].astype(F32)).astype(BF16)
+                    self.q[s, ab, s2] = (self.h[s, ab, s1, s2].astype(F32) + self.r1[s, ab, s2].astype(F32)).astype(BF16)
             for cp in self.second(b):
                 cp.start()
 
-        @pl.when(at(SECOND, ALL))
+        @pl.when(at(FIRST, gathered))
         def _():
-            for cp in self.second(t - SECOND):
+            first_stage(t - FIRST)
+
+        @pl.when(at(FIRST_LATE, ALL, gathered))
+        def _():
+            first_stage(t - FIRST_LATE)
+
+        @pl.when(at(SECOND, gathered))
+        def _():
+            b = t - SECOND
+            for cp in self.second(b):
                 cp.wait()
-
-        if gathered:
-
-            @pl.when(at(SECOND, gathered))
-            def _():
-                b = t - SECOND
-                self.sums(b, self.e.at[lax.rem(b, SLOTS)])
-                for cp in self.own(b) + self.back_first(b):
-                    cp.start()
+            self.sums(b, self.e.at[lax.rem(b, SLOTS)])
+            for cp in self.own(b) + self.back_first(b):
+                cp.start()
 
         for begin, end, e_ref in e_refs:
 
-            @pl.when(at(SECOND, end, begin))
+            @pl.when(at(SECOND_LATE, end, begin))
             def _(e_ref=e_ref):
-                self.sums(t - SECOND, e_ref.at[0])
+                b = t - SECOND_LATE
+                for cp in self.second(b):
+                    cp.wait()
+                self.sums(b, e_ref.at[0])
 
         if gathered:
 
@@ -314,8 +316,8 @@
 
 EXCHANGE_SCRATCH = [
     pltpu.VMEM((2, 2, 2, 2, 2, 3, 64, BLK), BF16),
-    pltpu.VMEM((2, 2, 2, 2, 3, 64, BLK), BF16),
-    pltpu.VMEM((2, 2, 2, 3, 64, BLK), BF16),
+    pltpu.VMEM((SLOTS, 2, 2, 2, 3, 64, BLK), BF16),
+    pltpu.VMEM((SLOTS, 2, 2, 3, 64, BLK), BF16),
     pltpu.VMEM((SLOTS, 2, 3, 64, BLK), BF16),
     pltpu.VMEM((SLOTS, 2, 2, 2, 3, 64, BLK), BF16),
     pltpu.VMEM((SLOTS, 2, 2, 3, 64, BLK), BF16),
@@ -326,7 +328,7 @@
     pltpu.SemaphoreType.REGULAR((3,)),
 ]
 ALL = 2 * NB
-STEPS = ALL + SECOND
+STEPS = ALL + SECOND_LATE
 HALF = 7
 
 
@@ -334,11 +336,11 @@
     slot = lax.rem(t, 2)
     store_pieces(ex.g, slot, 0, dot(at_ref[...], dg_s[...]))
     store_pieces(ex.g, slot, 1, dot(at_ref[...], du_s[...]))
-    store_pieces(ex.g, slot, 2, dot(dt_ref[...], hid_s[slot]).T)
+    store_pieces(ex.g, slot, 2, dot(dt_ref[...], hid_s[...]).T)
 
 
 def backward_kernel(
-    a_hbm, dy_hbm, dyt_hbm, h_hbm, a0t_hbm, by_gate_hbm, by_up_hbm, hid_hbm, wg_ref, wu_ref, wd_ref,
+    a_hbm, dy_hbm, dyt_hbm, h_hbm, a0t_hbm, gate_hbm, up_hbm, wg_ref, wu_ref, wd_ref,
     e0a_ref, e0b_ref, f_ref,
     a_s, at_s, d_s, dt_s, acc, g_s, u_s, dh_s, hid_s, dg_s, du_s, loads, *scratch,
 ):
@@ -350,11 +352,7 @@
 
     def load_hidden(step):
         cols = pl.ds(pl.multiple_of((step - NB) * BLK, BLK), BLK)
-        return [load(6, by_gate_hbm.at[:, cols], g_s), load(7, by_up_hbm.at[:, cols], u_s)]
-
-    def load_units(step):
-        cols = pl.ds(pl.multiple_of((step - NB) * BLK, BLK), BLK)
-        return load(8 + lax.rem(step, 2), hid_hbm.at[:, cols], hid_s.at[lax.rem(step, 2)])
+        return [load(6, gate_hbm.at[:, cols], g_s), load(7, up_hbm.at[:, cols], u_s)]
 
     load_a = load(0, a_hbm, a_s)
     other_loads = [load(1, dy_hbm, d_s), load(3, dyt_hbm, dt_s)]
@@ -383,10 +381,6 @@
     def _():
         ex.wait_peers()
 
-    @pl.when((t >= NB - 1) & (t < ALL - 1))
-    def _():
-        load_units(t + 1).start()
-
     @pl.when(t < NB)
     def _():
         def front(rows):
@@ -396,7 +390,7 @@
             dh_s[rows, :] = dot_nt(d_s[rows, :], wd_ref[0])
 
         def back(rows):
-            hid_s[lax.rem(t, 2), rows, :], by_gate, by_up = by_gate_and_up(g_s[rows, :], u_s[rows, :])
+            hid_s[rows, :], by_gate, by_up = by_gate_and_up(g_s[rows, :], u_s[rows, :])
             dh = dh_s[rows, :].astype(BF16).astype(F32)
             dgate = (dh * by_gate).astype(BF16)
             dup = (dh * by_up).astype(BF16)
@@ -435,7 +429,7 @@
 
     @pl.when((t >= NB) & (t < ALL))
     def _():
-        for cp in [*load_hidden(t), load_units(t)]:
+        for cp in load_hidden(t):
             cp.wait()
 
         def front(rows):
@@ -443,7 +437,7 @@
 
         def back(rows):
             dh = dh_s[rows, :].astype(BF16).astype(F32)
-            _, by_gate, by_up = by_gate_and_up(g_s[rows, :], u_s[rows, :])
+            hid_s[rows, :], by_gate, by_up = by_gate_and_up(g_s[rows, :], u_s[rows, :])
             dg_s[rows, :] = (dh * by_gate).astype(BF16)
             du_s[rows, :] = (dh * by_up).astype(BF16)
 
@@ -474,14 +468,14 @@
 
 
 def sums_spec(begin, end):
-    return pl.BlockSpec((1,) + PIECES, lambda t: (jnp.clip(t - SECOND - begin, 0, end - begin - 1), 0, 0, 0, 0))
+    return pl.BlockSpec((1,) + PIECES, lambda t: (jnp.clip(t - SECOND_LATE - begin, 0, end - begin - 1), 0, 0, 0, 0))
 
 
 def sums_shape(begin, end):
     return jax.ShapeDtypeStruct((end - begin,) + PIECES, BF16)
 
 
-def backward(a, dy, dyt, h, a0t, by_gate, by_up, hid, wg, wu, wd):
+def backward(a, dy, dyt, h, a0t, gate, up, wg, wu, wd):
     any_spec = pl.BlockSpec(memory_space=pl.ANY)
     wide = pl.BlockSpec((1, D, BLK), lambda t: (1, 0, jnp.minimum(t, NB - 1)))
     tall = pl.BlockSpec((1, BLK, D), lambda t: (jnp.where(t < NB, 1, 0), jnp.where(t < NB, t, jnp.minimum(t, ALL - 1) - NB), 0))
@@ -489,7 +483,7 @@
     return pl.pallas_call(
         backward_kernel,
         grid=(STEPS,),
-        in_specs=[any_spec] * 8 + [wide, wide, tall],
+        in_specs=[any_spec] * 7 + [wide, wide, tall],
         out_specs=[*[sums_spec(*e) for e in ends], any_spec],
         out_shape=[*[sums_shape(*e) for e in ends], jax.ShapeDtypeStruct((NB,) + FULL, BF16)],
         scratch_shapes=[
@@ -499,15 +493,14 @@
             pltpu.VMEM((D, T), BF16),
             pltpu.VMEM((T, D), F32),
             *[pltpu.VMEM((T, BLK), F32)] * 3,
-            pltpu.VMEM((2, T, BLK), BF16),
-            *[pltpu.VMEM((T, BLK), BF16)] * 2,
-            pltpu.SemaphoreType.DMA((10,)),
+            *[pltpu.VMEM((T, BLK), BF16)] * 3,
+            pltpu.SemaphoreType.DMA((8,)),
             *EXCHANGE_SCRATCH,
         ],
         compiler_params=pltpu.CompilerParams(vmem_limit_bytes=VMEM_LIMIT, collective_id=0, has_side_effects=True),
         cost_estimate=pl.CostEstimate(flops=24 * T * D * FF, bytes_accessed=12 * T * FF, transcendentals=2 * T * FF),
         name="backward",
-    )(a, dy, dyt, h, a0t, by_gate, by_up, hid, wg, wu, wd)
+    )(a, dy, dyt, h, a0t, gate, up, wg, wu, wd)
 
 
 def adamw(w, m, v, g):
@@ -561,8 +554,8 @@
 def solution(mesh):
     def step(x, dy, wg, wu, wd, *moments):
         x, dy = x[0], dy[0]
-        by_gate, by_up, hid, h1, a1, a0t, dyt = forward(x, dy, wg, wu, wd)
-        e0a, e0b, f1 = backward(a1, dy, dyt, h1, a0t, by_gate, by_up, hid, wg, wu, wd)
+        gate, up, h1, a1, a0t, dyt = forward(x, dy, wg, wu, wd)
+        e0a, e0b, f1 = backward(a1, dy, dyt, h1, a0t, gate, up, wg, wu, wd)
         g0a, g0b = (lax.all_gather(e, "dp", axis=0, tiled=False) for e in (e0a, e0b))
         arrays = (wg, wu, wd, *moments)
         new = update(1, 0, f1, arrays, None)

time: 515 us -> 512 us (level)
  transfers between devices with their start and end apart: 2 -> 2, of which waited for: 0 -> 0; matrix products, arithmetic and copies ran while one was open for 0% -> 0% of each run, Pallas kernels for 22% -> 23%
where the time goes in v4:
time: 512 us; the launch traced here: 511 us
  Pallas kernels  496 us (97%)
  between operations  14.1 us (3%)
    pallas_call x1, Pallas kernels, backward(): pl.pallas_call(backward_kernel, grid=(STEPS,), in_specs=[any_spec] * 7 +...  290 us
    pallas_call x3, Pallas kernels, update(): pl.pallas_call(functools.partial(adamw_kernel, own), grid=(count,), in_sp...  149 us
    pallas_call x1, Pallas kernels, forward(): pl.pallas_call(forward_kernel, grid=(NB,), in_specs=[whole((T, D)), pl.Bl...  57.7 us
  transfers between devices with their start and end apart: 2, of which 0 were waited for; matrix products, arithmetic and copies ran while one was open for 0% of the time, Pallas kernels for 23%

profile of v4, /device:TPU:0, one launch (start us, length us, event | category | flops | bytes accessed | tf_op | source)
XLA Modules:
  0.0 511.4 jit_solution(11520513442802631290)
XLA Ops:
  7.2 0.0 all-gather.7.cloned.1.call-start
  7.2 57.7 %fwd0.1 = (f32[2048,3328]{1,0:T(8,128)}, f32[2048,3328]{1,0:T(8,128)}, bf16[2048,1024]{1,0:T(8,128)(2,1)}, bf16[2048,1024]{1,0:T(8,128)(2,1)}, bf16[1024,2048]{1,0:T(8,128)(2,1)}, /*index=5*/bf16[1024,2048]{1,0:T(8,128)(2,1)}) custom-call(bf16[2048,1024]{1,0:T(8,128)(2,1)} %bitcast.6, bf16[2048,1024]{1,0:T(8,128)(2,1)} %bitcast.7, ...), custom_call_target="tpu_custom_call" | custom-call | flops 41875931136 | bytes 54525952 | tf_op jit(solution)/shard_map/fwd0/pallas_call | solution.py:103
  64.9 289.9 %backward.1 = (bf16[7,2,3,64,256]{4,3,2,1,0:T(8,128)(2,1)}, bf16[6,2,3,64,256]{4,3,2,1,0:T(8,128)(2,1)}, bf16[13,2,2,2,2,3,64,256]{7,6,5,4,3,2,1,0:T(8,128)(2,1)}) custom-call(bf16[2048,1024]{1,0:T(8,128)(2,1)} %get-tuple-element.36.a_hbm, bf16[2048,1024]{1,0:T(8,128)(2,1)} %bitcast.8, bf16[1024,2048]{1,0:T(8,128)(2,1)} %get-tuple-element.37.dyt_hbm, ...), custom_call_target="tpu_custom_call" | custom-call | flops 167503724544 | bytes 81788928 | tf_op jit(solution)/shard_map/backward/pallas_call | solution.py:483
  354.8 0.0 all-gather.7.cloned.1.call-update
  354.8 0.0 all-gather.5.cloned.1.call-start
  354.9 0.7 all-gather.5.cloned.1.call-update
  355.6 74.2 %adamw1_0.1 = (bf16[2,1024,3328]{2,1,0:T(8,128)(2,1)}, bf16[2,1024,3328]{2,1,0:T(8,128)(2,1)}, bf16[2,3328,1024]{2,1,0:T(8,128)(2,1)}, f32[2,1024,3328]{2,1,0:T(...) custom-call(bf16[13,2,2,2,2,3,64,256]{7,6,5,4,3,2,1,0:T(8,128)(2,1)}, ...), custom_call_target="tpu_custom_call" | custom-call | flops 306708480 | bytes 224919552 | tf_op jit(solution)/shard_map/adamw1_0/pallas_call | solution.py:541
  429.8 0.0 all-gather.7.cloned.1.call-done
  429.9 41.5 %adamw0_0.1 = (bf16[2,1024,3328]{2,1,0:T(8,128)(2,1)}, bf16[2,1024,3328]{2,1,0:T(8,128)(2,1)}, bf16[2,3328,1024]{2,1,0:T(8,128)(2,1)}, f32[2,1024,3328]{2,1,0:T(...) custom-call(bf16[8,7,2,3,64,256]{5,4,3,2,1,0:T(8,128)(2,1)} %bitcast, ...), custom_call_target="tpu_custom_call", output_to_operand_aliasing={{0}: (10, {}), {1}: (11, {}), {2}: (12, {}), {3}: (13, {}),... | custom-call | flops 165150720 | bytes 121110528 | tf_op jit(solution)/shard_map/adamw0_0/pallas_call | solution.py:541
  471.4 0.0 all-gather.5.cloned.1.call-done
  471.4 33.1 %adamw0_7.1 = (bf16[2,1024,3328]{2,1,0:T(8,128)(2,1)}, bf16[2,1024,3328]{2,1,0:T(8,128)(2,1)}, bf16[2,3328,1024]{2,1,0:T(8,128)(2,1)}, f32[2,1024,3328]{2,1,0:T(...) custom-call(bf16[8,6,2,3,64,256]{5,4,3,2,1,0:T(8,128)(2,1)} %bitcast, ...), custom_call_target="tpu_custom_call", output_to_operand_aliasing={{0}: (10, {}), {1}: (11, {}), {2}: (12, {}), {3}: (13, {}),... | custom-call | flops 141557760 | bytes 103809024 | tf_op jit(solution)/shard_map/adamw0_7/pallas_call | solution.py:541
Async XLA Ops:
  7.2 422.7 %all-gather.7.cloned.1.call-start = ((), (), s32[]{:S(2)}) async-start(), calls=%async_computation.1 | async-start | bytes 12386304 | tf_op jit(solution)/shard_map/all_gather | solution.py:559
  354.8 116.5 %all-gather.5.cloned.1.call-start = ((), (), s32[]{:S(2)}) async-start(), calls=%async_computation | async-start | bytes 10616832 | tf_op jit(solution)/shard_map/all_gather | solution.py:559
Sparse Core Ops, SparseCore 0:
  355.0 59.6 all-gather.6
  416.4 52.9 all-gather.4
